TPU v7x, 128 devices: a whole 4x4x4 slice. The times are simulated.
128 devices in a mesh: lat: 64 (over z, x, y), head: 2 (over core).
Axes of the slice: x: 4, y: 4, z: 4, core: 2. Of those that a mesh axis runs over, the one named last changes fastest.
Arguments:
- grid_latent: bfloat16 [524288, 512], P('lat'), may hold values from -6 to 6
- mesh_latent: bfloat16 [40960, 512], P('lat'), may hold values from -6 to 6
- neighbours: int32 [40960, 16], P('lat'), may hold values from -1 to 524287, as said below
- edge_bias: bfloat16 [40960, 64], P('lat', 'head'), may hold values from -8 to 384
- query_weight: bfloat16 [512, 512], P(None, 'head'), may hold values from -0.25 to 0.25
- key_weight: bfloat16 [512, 512], P(None, 'head'), may hold values from -0.25 to 0.25
- value_weight: bfloat16 [512, 512], P(None, 'head'), may hold values from -0.25 to 0.25
- out_weight: bfloat16 [512, 512], P('head'), may hold values from -0.25 to 0.25
- norm_gain: bfloat16 [512], P('head'), may hold values from 0.5 to 1.5
Outputs:
- mesh_out: bfloat16 [40960, 512], P('lat', 'head')
Inputs may be any that keep to these rules, and one draw needn't show every extreme that they name: `neighbours`: every neighbour of mesh node m is -1 or lies in [b * 8192 - 2048, (b + 1) * 8192 + 2048) with b = m // 640; both ends of that range (cut to the grid) are named in every draw; slots 0 and 1 are never -1.
All inputs are finite; a program needn't handle non-finite values.
Results may differ from a plain program's by a relative error of at most 0.0075.
Values may be sent and summed in bfloat16 or wider, within the bound.
A program may use at most 128 MiB of HBM per device.

v0:
```python
import jax
import jax.numpy as jnp
from jax import lax
from jax.sharding import PartitionSpec as P

D = 512
K = 16
HEAD_DIM = 128
HALO = 2048


EPSILON = 1e-05


def extended(block, sides, width):
    for axis, dim in sides:
        count = lax.axis_size(axis)
        forward = [(i, i + 1) for i in range(count - 1)]
        backward = [(target, source) for source, target in forward]
        low = lax.ppermute(
            lax.slice_in_dim(block, block.shape[dim] - width, None, axis=dim), axis, forward
        )
        high = lax.ppermute(lax.slice_in_dim(block, 0, width, axis=dim), axis, backward)
        block = jnp.concatenate([low, block, high], axis=dim)
    return block


def sent_to_all(shard, axis):
    copies = jnp.broadcast_to(shard, (lax.axis_size(axis), *shard.shape))
    return lax.all_to_all(copies, axis, split_axis=0, concat_axis=0, tiled=True)


def of_everyone(shard, axis):
    return sent_to_all(shard, axis).astype(jnp.float32).sum(axis=0)


def partial_softmax(queries, bias_rows, valid, local, keys, values, local_heads):
    count = queries.shape[0]
    safe_rows = jnp.where(valid, local, 0).reshape(-1)
    key_rows = (
        jnp.take(keys, safe_rows, axis=0)
        .reshape(count, K, local_heads, HEAD_DIM)
        .astype(jnp.float32)
    )
    value_rows = (
        jnp.take(values, safe_rows, axis=0)
        .reshape(count, K, local_heads, HEAD_DIM)
        .astype(jnp.float32)
    )
    query_heads = queries.astype(jnp.float32).reshape(count, local_heads, HEAD_DIM)
    scores = jnp.einsum("nhc,nkhc->nhk", query_heads, key_rows) * HEAD_DIM ** (-0.5)
    scores = scores + bias_rows.astype(jnp.float32).reshape(count, local_heads, K)
    live = valid[:, None, :]
    scores = jnp.where(live, scores, -1e30)
    top_score = jnp.max(scores, axis=2)
    weights = jnp.where(live, jnp.exp(scores - top_score[:, :, None]), 0.0)
    total = jnp.sum(weights, axis=2)
    summed = jnp.einsum("nhk,nkhc->nhc", weights, value_rows)
    return (top_score, total, summed)


def shards(
    grid_latent,
    mesh_latent,
    neighbours,
    edge_bias,
    query_weight,
    key_weight,
    value_weight,
    out_weight,
    norm_gain,
):
    band = grid_latent.shape[0]
    count = mesh_latent.shape[0]
    local_width = key_weight.shape[1]
    local_heads = local_width // HEAD_DIM
    lat_pos = lax.axis_index("lat")
    keys = jnp.dot(grid_latent, key_weight, preferred_element_type=jnp.float32).astype(jnp.bfloat16)
    values = jnp.dot(grid_latent, value_weight, preferred_element_type=jnp.float32).astype(
        jnp.bfloat16
    )
    queries = jnp.dot(mesh_latent, query_weight, preferred_element_type=jnp.float32).astype(
        jnp.bfloat16
    )
    wide_keys, wide_values = (
        extended(keys, (("lat", 0),), HALO),
        extended(values, (("lat", 0),), HALO),
    )
    offset = lat_pos * band - HALO
    valid = neighbours >= 0
    local = jnp.where(valid, neighbours - offset, -1)
    top_score, total, summed = partial_softmax(
        queries, edge_bias, valid, local, wide_keys, wide_values, local_heads
    )
    mixed = summed / total[:, :, None]
    attended = mixed.reshape(count, local_width).astype(jnp.bfloat16)
    projected = jnp.dot(attended, out_weight, preferred_element_type=jnp.float32)
    start = lax.axis_index("head") * local_width
    combined = of_everyone(projected.astype(jnp.bfloat16), "head").astype(jnp.float32)
    updated_full = mesh_latent.astype(jnp.float32) + combined
    row_sums = jnp.sum(updated_full, axis=1)
    row_squares = jnp.sum(updated_full * updated_full, axis=1)
    updated = lax.dynamic_slice_in_dim(updated_full, start, local_width, 1)
    mean = row_sums / D
    variance = row_squares / D - mean * mean
    normed = (
        (updated - mean[:, None])
        * lax.rsqrt(variance[:, None] + EPSILON)
        * norm_gain.astype(jnp.float32)
    )
    return normed.astype(jnp.bfloat16)


def solution(mesh):
    in_specs = (
        P("lat", None),
        P("lat", None),
        P("lat", None),
        P("lat", "head"),
        P(None, "head"),
        P(None, "head"),
        P(None, "head"),
        P("head", None),
        P("head"),
    )
    out_specs = P("lat", "head")
    return jax.shard_map(shards, mesh=mesh, in_specs=in_specs, out_specs=out_specs, check_vma=False)
```

profile of v0, /device:TPU:97, one launch (start us, length us, event | category | flops | bytes accessed | tf_op | source)
XLA Modules:
  0.0 206.8 jit_solution(1372123821433578798)
XLA Ops:
  0.0 0.9 copy-done
  1.0 6.1 %convolution_convert_fusion.1 = bf16[8192,256]{1,0:T(8,128)(2,1)S(1)} fusion(bf16[8192,512]{1,0:T(8,128)(2,1)} %param.11, bf16[512,256]{1,0:T(8,128)(2,1)S(1)} %copy-done), kind=kOutput, calls=%fused_computation.5 | convolution fusion | flops 2149580800 | bytes 12845056 | tf_op jit(solution)/shard_map/dot_general | solution.py:78
  7.1 1.6 fusion.19
  8.6 3.2 %collective-permute-start = (bf16[2048,256]{1,0:T(8,128)(2,1)}, bf16[2048,256]{1,0:T(8,128)(2,1)}, u32[]{:S(2)}, u32[]{:S(2)}) collective-permute-start(bf16[2048,256]{1,0:T(8,128)(2,1)} %get-tuple-element.11), channel_id=1, source_target_pairs={{0,2},{2,4},{4,6},{6,8},{8,10},{10,12},{12,14},{14,16},{16,18},{18... | collective-permute-start | bytes 3145736 | tf_op jit(solution)/shard_map/ppermute | solution.py:20
  11.9 6.4 %collective-permute-start.1 = (bf16[2048,256]{1,0:T(8,128)(2,1)}, bf16[2048,256]{1,0:T(8,128)(2,1)}, u32[]{:S(2)}, u32[]{:S(2)}) collective-permute-start(bf16[2048,256]{1,0:T(8,128)(2,1)} %get-tuple-element.12), channel_id=1, source_target_pairs={{2,0},{4,2},{6,4},{8,6},{10,8},{12,10},{14,12},{16,14},{18,16},{20... | collective-permute-start | bytes 3145736 | tf_op jit(solution)/shard_map/ppermute | solution.py:23
  18.3 2.3 %convolution_convert_fusion = bf16[8192,256]{1,0:T(8,128)(2,1)S(1)} fusion(bf16[8192,512]{1,0:T(8,128)(2,1)S(1)} %copy-done.8, bf16[512,256]{1,0:T(8,128)(2,1)S(1)} %copy-done.9), kind=kOutput, calls=%fused_computation.4 | convolution fusion | flops 2149580800 | bytes 12845056 | tf_op jit(solution)/shard_map/dot_general | solution.py:79
  20.7 2.0 copy-done.2
  22.7 1.5 fusion.18
  24.2 1.9 collective-permute-start.2
  26.1 7.6 %collective-permute-start.3 = (bf16[2048,256]{1,0:T(8,128)(2,1)}, bf16[2048,256]{1,0:T(8,128)(2,1)}, u32[]{:S(2)}, u32[]{:S(2)}) collective-permute-start(bf16[2048,256]{1,0:T(8,128)(2,1)} %get-tuple-element.10), channel_id=1, source_target_pairs={{2,0},{4,2},{6,4},{8,6},{10,8},{12,10},{14,12},{16,14},{18,16},{20... | collective-permute-start | bytes 3145736 | tf_op jit(solution)/shard_map/ppermute | solution.py:23
  34.1 0.4 convolution_convert_fusion.3
  34.5 0.9 copy.25
  35.5 3.6 %collective-permute-done = bf16[2048,256]{1,0:T(8,128)(2,1)} collective-permute-done((bf16[2048,256]{1,0:T(8,128)(2,1)}, bf16[2048,256]{1,0:T(8,128)(2,1)}, u32[]{:S(2)}, u32[]{:S(2)}) %collective-permute-start) | collective-permute-done | bytes 1048608 | tf_op jit(solution)/shard_map/ppermute | solution.py:20
  39.1 1.1 collective-permute-done.1
  40.2 8.6 %pad_maximum_fusion = bf16[12288,256]{1,0:T(8,128)(2,1)} fusion(bf16[2048,256]{1,0:T(8,128)(2,1)} %collective-permute-done.1, bf16[8192,256]{1,0:T(8,128)(2,1)} %copy-done.3, bf16[2048,256]{1,0:T(8,128)(2,1)} %collective-permute-done), kind=kLoop, calls=%fused_computation.6 | loop fusion | flops 18874368 | bytes 12582912 | tf_op jit(solution)/shard_map/concatenate | solution.py:24
  48.8 42.1 %gather_fusion = bf16[10240,256]{1,0:T(8,128)(2,1)} fusion(bf16[12288,256]{1,0:T(8,128)(2,1)} %pad_maximum_fusion, s32[10240]{0:T(1024)S(1)} %fusion.14), kind=kCustom, calls=%fused_computation.clone | custom fusion | bytes 10526720 | tf_op jit(solution)/shard_map/jit(_take)/gather | solution.py:41
  90.9 12.0 %pad_maximum_fusion.1 = bf16[12288,256]{1,0:T(8,128)(2,1)} fusion(bf16[2048,256]{1,0:T(8,128)(2,1)} %collective-permute-done.3, bf16[8192,256]{1,0:T(8,128)(2,1)} %copy-done.2, bf16[2048,256]{1,0:T(8,128)(2,1)S(1)} %collective-permute-done.2), kind=kLoop, calls=%fused_computation.7 | loop fusion | flops 18874368 | bytes 12582912 | tf_op jit(solution)/shard_map/concatenate | solution.py:24
  102.9 42.2 %gather_fusion.1 = bf16[10240,256]{1,0:T(8,128)(2,1)} fusion(bf16[12288,256]{1,0:T(8,128)(2,1)} %pad_maximum_fusion.1, s32[10240]{0:T(1024)S(1)} %fusion.14), kind=kCustom, calls=%fused_computation.1.clone | custom fusion | bytes 10526720 | tf_op jit(solution)/shard_map/jit(_take)/gather | solution.py:46
  145.1 10.6 %broadcast_select_fusion = (bf16[10240,256]{1,0:T(8,128)(2,1)}, bf16[10240,256]{1,0:T(8,128)(2,1)}) fusion(bf16[10240,256]{1,0:T(8,128)(2,1)} %gather_fusion.1, pred[10240]{0:T(1024)(128)(4,1)S(1)} %compare_and_fusion, bf16[10240,256]{1,0:T(8,128)(2,1)} %gather_fusion), kind=kLoop, calls=%fused_computation.10 | loop fusion | flops 5242880 | bytes 20981760 | tf_op jit(solution)/shard_map/jit(_take)/select_n | solution.py:46
  155.7 8.3 %reshape.45 = bf16[640,16,2,128]{3,2,1,0:T(2,128)(2,1)} reshape(bf16[10240,256]{1,0:T(8,128)(2,1)} %get-tuple-element.14) | data formatting | bytes 10485760 | tf_op jit(solution)/shard_map/reshape | solution.py:42
  164.0 15.3 %multiply_reduce_fusion = f32[640,2,16]{1,2,0:T(8,128)} fusion(f32[640,2,128]{2,1,0:T(2,128)S(1)} %copy.25, bf16[640,16,2,128]{3,2,1,0:T(2,128)(2,1)} %reshape.45), kind=kLoop, calls=%fused_computation.3 | loop fusion | flops 7843840 | bytes 5980160
  179.3 3.3 %copy.21 = f32[640,2,16]{0,2,1:T(8,128)S(1)} copy(f32[640,2,16]{1,2,0:T(8,128)} %multiply_reduce_fusion) | data formatting | bytes 163840 | tf_op jit(solution)/shard_map/nhc,nkhc->nhk/dot_general | solution.py:51
  182.7 0.9 copy.22
  183.5 8.5 %reshape.48 = bf16[640,16,2,128]{3,2,1,0:T(2,128)(2,1)} reshape(bf16[10240,256]{1,0:T(8,128)(2,1)} %get-tuple-element.13) | data formatting | bytes 10485760 | tf_op jit(solution)/shard_map/reshape | solution.py:47
  192.1 0.2 copy.14
  192.3 4.0 %fusion.1 = f32[640,2,1,128]{3,2,1,0:T(1,128)S(1)} fusion(bf16[640,2,16,1]{2,3,1,0:T(2,128)(2,1)S(1)} %copy.22, bf16[640,16,2,128]{3,2,1,0:T(2,128)(2,1)} %reshape.48), kind=kOutput, calls=%fused_computation.8 | convolution fusion | flops 5242880 | bytes 5939200 | tf_op jit(solution)/shard_map/nhk,nkhc->nhc/dot_general | solution.py:58
  196.2 0.9 divide_convert_fusion
  197.1 0.3 convolution_convert_fusion.2
  197.6 7.6 %all_to_all.5 = bf16[2,640,512]{2,1,0:T(8,128)(2,1)S(1)} all-to-all(bf16[2,640,512]{2,1,0:T(8,128)(2,1)S(1)} %broadcast_in_dim.45), channel_id=1, replica_groups=mesh['lat'=64,'head'=2] {'head'}, dimensions={0} | all-to-all | bytes 2621440 | tf_op jit(solution)/shard_map/all_to_all | solution.py:30
  205.2 0.3 convert_reduce_fusion
  205.5 0.3 fusion.17
  205.8 1.0 multiply_convert_fusion
  (34 shorter events, 0.6 us)
Async XLA Ops:
  0.0 1.0 copy-start
  0.0 18.3 %copy-start.8 = (bf16[8192,512]{1,0:T(8,128)(2,1)S(1)}, bf16[8192,512]{1,0:T(8,128)(2,1)}, u32[]{:S(2)}) copy-start(bf16[8192,512]{1,0:T(8,128)(2,1)} %param.11) | copy-start | bytes 25165828
  0.0 18.3 %copy-start.9 = (bf16[512,256]{1,0:T(8,128)(2,1)S(1)}, bf16[512,256]{1,0:T(8,128)(2,1)}, u32[]{:S(2)}) copy-start(bf16[512,256]{1,0:T(8,128)(2,1)} %param.17) | copy-start | bytes 786436
  7.1 4.8 %copy-start.3 = (bf16[8192,256]{1,0:T(8,128)(2,1)}, bf16[8192,256]{1,0:T(8,128)(2,1)S(1)}, u32[]{:S(2)}) copy-start(bf16[8192,256]{1,0:T(8,128)(2,1)S(1)} %convolution_convert_fusion.1) | copy-start | bytes 12582916
  8.6 30.5 %collective-permute-start = (bf16[2048,256]{1,0:T(8,128)(2,1)}, bf16[2048,256]{1,0:T(8,128)(2,1)}, u32[]{:S(2)}, u32[]{:S(2)}) collective-permute-start(bf16[2048,256]{1,0:T(8,128)(2,1)} %get-tuple-element.11), channel_id=1, source_target_pairs={{0,2},{2,4},{4,6},{6,8},{8,10},{10,12},{12,14},{14,16},{16,18},{18... | collective-permute-start | bytes 3145736 | tf_op jit(solution)/shard_map/ppermute | solution.py:20
  11.9 21.8 %copy-start.7 = (s32[640,16]{0,1:T(8,128)S(1)}, s32[640,16]{0,1:T(8,128)}, u32[]{:S(2)}) copy-start(s32[640,16]{0,1:T(8,128)} %param.13) | copy-start | bytes 122884
  11.9 22.2 %copy-start.5 = (bf16[512,256]{1,0:T(8,128)(2,1)S(1)}, bf16[512,256]{1,0:T(8,128)(2,1)}, u32[]{:S(2)}) copy-start(bf16[512,256]{1,0:T(8,128)(2,1)} %param.15) | copy-start | bytes 786436
  11.9 28.3 %collective-permute-start.1 = (bf16[2048,256]{1,0:T(8,128)(2,1)}, bf16[2048,256]{1,0:T(8,128)(2,1)}, u32[]{:S(2)}, u32[]{:S(2)}) collective-permute-start(bf16[2048,256]{1,0:T(8,128)(2,1)} %get-tuple-element.12), channel_id=1, source_target_pairs={{2,0},{4,2},{6,4},{8,6},{10,8},{12,10},{14,12},{16,14},{18,16},{20... | collective-permute-start | bytes 3145736 | tf_op jit(solution)/shard_map/ppermute | solution.py:23
  20.7 2.0 copy-start.2
  22.7 11.3 %copy-start.4 = (bf16[640,512]{1,0:T(8,128)(2,1)S(1)}, bf16[640,512]{1,0:T(8,128)(2,1)}, u32[]{:S(2)}) copy-start(bf16[640,512]{1,0:T(8,128)(2,1)} %param.12) | copy-start | bytes 1966084
  22.7 12.6 %copy-start.11 = (bf16[256]{0:T(256)(128)(2,1)S(1)}, bf16[256]{0:T(256)(128)(2,1)}, u32[]{:S(2)}) copy-start(bf16[256]{0:T(256)(128)(2,1)} %param.19) | copy-start | bytes 1540
  24.2 66.7 %collective-permute-start.2 = (bf16[2048,256]{1,0:T(8,128)(2,1)}, bf16[2048,256]{1,0:T(8,128)(2,1)S(1)}, u32[]{:S(2)}, u32[]{:S(2)}) collective-permute-start(bf16[2048,256]{1,0:T(8,128)(2,1)} %get-tuple-element.9), channel_id=1, source_target_pairs={{0,2},{2,4},{4,6},{6,8},{8,10},{10,12},{12,14},{14,16},{16,18},{18... | collective-permute-start | bytes 3145736 | tf_op jit(solution)/shard_map/ppermute | solution.py:20
  26.1 64.8 %collective-permute-start.3 = (bf16[2048,256]{1,0:T(8,128)(2,1)}, bf16[2048,256]{1,0:T(8,128)(2,1)}, u32[]{:S(2)}, u32[]{:S(2)}) collective-permute-start(bf16[2048,256]{1,0:T(8,128)(2,1)} %get-tuple-element.10), channel_id=1, source_target_pairs={{2,0},{4,2},{6,4},{8,6},{10,8},{12,10},{14,12},{16,14},{18,16},{20... | collective-permute-start | bytes 3145736 | tf_op jit(solution)/shard_map/ppermute | solution.py:23
  179.3 3.3 %copy-start.10 = (bf16[640,32]{0,1:T(8,128)(2,1)S(1)}, bf16[640,32]{0,1:T(8,128)(2,1)}, u32[]{:S(2)}) copy-start(bf16[640,32]{0,1:T(8,128)(2,1)} %param.14) | copy-start | bytes 122884
  192.1 5.0 %copy-start.6 = (bf16[256,512]{1,0:T(8,128)(2,1)S(1)}, bf16[256,512]{1,0:T(8,128)(2,1)}, u32[]{:S(2)}) copy-start(bf16[256,512]{1,0:T(8,128)(2,1)} %param.18) | copy-start | bytes 786436
  197.5 9.3 %copy-start.1 = (bf16[512,256]{1,0:T(8,128)(2,1)S(1)}, bf16[512,256]{1,0:T(8,128)(2,1)}, u32[]{:S(2)}) copy-start(bf16[512,256]{1,0:T(8,128)(2,1)} %param.16) | copy-start | bytes 786436
where the time goes:
time: 210 us; the launch traced here: 207 us
  local copies, waits for them, and re-layouts  113 us (54%)
  other arithmetic  49 us (23%)
  starting transfers between devices  19.1 us (9%)
  matrix products  13.2 us (6%)
  blocking collectives  7.63 us (4%)
  waiting for transfers between devices  4.72 us (2%)
    gather x1, local copies, waits for them, and re-layouts, partial_softmax(): jnp.take(values, safe_rows, axis=0).reshape(count, K, local_heads, HEAD_DIM)  42.2 us
    gather x1, local copies, waits for them, and re-layouts, partial_softmax(): jnp.take(keys, safe_rows, axis=0).reshape(count, K, local_heads, HEAD_DIM)  42.1 us
    concatenate x2, other arithmetic, extended(): block = jnp.concatenate([low, block, high], axis=dim)  20.6 us
    unnamed x1, other arithmetic  15.3 us
    ppermute x2, starting transfers between devices, extended(): lax.ppermute(lax.slice_in_dim(block, 0, width, axis=dim), axis, backward)  14 us
    select_n x1, other arithmetic, partial_softmax(): jnp.take(values, safe_rows, axis=0).reshape(count, K, local_heads, HEAD_DIM)  10.6 us
    reshape x1, local copies, waits for them, and re-layouts, partial_softmax(): value_rows = jnp.take(values, safe_rows, axis=0).reshape(count, K, local_...  8.54 us
    reshape x1, local copies, waits for them, and re-layouts, partial_softmax(): key_rows = jnp.take(keys, safe_rows, axis=0).reshape(count, K, local_head...  8.32 us
  transfers between devices with their start and end apart: 4, of which 2 were waited for; matrix products, arithmetic and copies ran while one was open for 27% of the time, Pallas kernels for 0%

commit v1 on v0

v1 whole, which is shorter than its diff:
```python
import functools

import jax
import jax.numpy as jnp
from jax import lax
from jax.experimental import pallas as pl
from jax.experimental.pallas import tpu as pltpu
from jax.sharding import PartitionSpec as P

D = 512
K = 16
HEADS = 4
HEAD_DIM = 128
HALO = 2048
EPSILON = 1e-05
TN = 32
CH = 512
DEAD = -1e30
VMEM = pl.BlockSpec(memory_space=pltpu.VMEM)
SMEM = pl.BlockSpec(memory_space=pltpu.SMEM)
ANY = pl.BlockSpec(memory_space=pl.ANY)
NT = (((1,), (1,)), ((), ()))
F32 = jnp.float32
BF16 = jnp.bfloat16


def compact_kernel(nb_ref, bias_ref, idx_ref, same_ref, cross_ref, *, band):
    first = lax.axis_index("head") == 0
    offset = lax.axis_index("lat") * band
    local = [nb_ref[k] - offset for k in range(K)]
    live = [nb_ref[k] >= 0 for k in range(K)]
    up = [local[k] >= band for k in range(K)]
    down = [live[k] & (local[k] < 0) for k in range(K)]
    for same in (True, False):
        use_up = first if same else jnp.logical_not(first)
        rank = []
        count = jnp.zeros(local[0].shape, jnp.int32)
        for k in range(K):
            here = jnp.where(use_up, up[k].astype(jnp.int32), down[k].astype(jnp.int32))
            rank.append(jnp.where(here > 0, count, -1))
            count = count + here
        shift = jnp.where(use_up, -band, HALO)
        out = same_ref if same else cross_ref
        for r in range(K):
            row = jnp.zeros(local[0].shape, jnp.int32)
            biases = [jnp.full(local[0].shape, DEAD, F32) for _ in range(2)]
            for k in range(r, K):
                hit = rank[k] == r
                if same:
                    row = jnp.where(hit, (local[k] + shift) * 4, row)
                for h in range(2):
                    biases[h] = jnp.where(hit, bias_ref[h * K + k], biases[h])
            if same:
                idx_ref[r] = row
            for h in range(2):
                out[h * K + r] = biases[h]


def compact(nb, bias, band):
    shape = nb.shape
    return pl.pallas_call(
        functools.partial(compact_kernel, band=band),
        out_shape=(
            jax.ShapeDtypeStruct(shape, jnp.int32),
            jax.ShapeDtypeStruct((2 * K,) + shape[1:], F32),
            jax.ShapeDtypeStruct((2 * K,) + shape[1:], F32),
        ),
        in_specs=[VMEM] * 2,
        out_specs=(VMEM,) * 3,
    )(nb, bias)


def attend_kernel(
    tiles, slots, rows, side, grid_ref, idx_ref, over_ref, bias_ref, mesh_ref, w_ref, v_ref, att_ref, lse_ref,
    buf, sems, table, st0, st1, qs, cs, gs, ss,
):
    edges = slots * TN
    base = lax.axis_index("head") * side
    chunks = rows // CH
    copies = [
        pltpu.make_async_copy(
            grid_ref.at[pl.ds(pl.multiple_of(base + i * CH, CH), CH), :], buf.at[pl.ds(i * CH, CH), :], sems.at[i]
        )
        for i in range(chunks)
    ]
    for copy in copies:
        copy.start()
    for pair in range(2):
        wq = w_ref[pair, :, 0:256]
        wk = w_ref[pair, :, 256:512]
        q = jnp.dot(mesh_ref[...], wq, preferred_element_type=F32).astype(BF16)
        for j in range(2):
            s = slice(j * HEAD_DIM, (j + 1) * HEAD_DIM)
            qk = lax.dot_general(q[:, s], wk[:, s], NT, preferred_element_type=F32)
            qs[2 * pair + j] = (qk * HEAD_DIM ** -0.5).astype(BF16)
    for i in range(chunks):
        copies[i].wait()
        for c in range(4):
            table[pl.ds(i * CH * 4 + c, CH, stride=4), :] = buf[pl.ds(i * CH, CH), c * 128:(c + 1) * 128].astype(F32)

    def same(width):
        node = lax.broadcasted_iota(jnp.int32, (TN, width), 0)
        lane = lax.broadcasted_iota(jnp.int32, (TN, width), 1)
        return (lane % TN) == node

    def gather(t, st, count):
        for p in range(count):
            st[pl.ds(4 * p, 4), :] = table[pl.ds(pl.multiple_of(idx_ref[t * (K * TN) + p], 4), 4), :]

    def staged(st, count):
        return jnp.concatenate([st[pl.ds(c, count, stride=4), :].astype(BF16) for c in range(4)], axis=1)

    def scores(t, g):
        r0 = pl.multiple_of(t * TN, TN)
        qt = jnp.concatenate([qs[h, pl.ds(r0, TN), :] for h in range(HEADS)], axis=0)
        sc = lax.dot_general(qt, g, NT, preferred_element_type=F32)
        mask = same(g.shape[0])
        return jnp.concatenate(
            [jnp.sum(jnp.where(mask, sc[h * TN:(h + 1) * TN], 0.0), axis=0, keepdims=True) for h in range(HEADS)], axis=0
        )

    def softmax(s):
        width = s.shape[1]

        def fold(x, op):
            y = x[:, 0:128]
            for j in range(1, width // 128):
                y = op(y, x[:, j * 128:(j + 1) * 128])
            y = op(y, pltpu.roll(y, 64, 1))
            return op(y, pltpu.roll(y, 32, 1))

        m = fold(s, jnp.maximum)
        w = jnp.exp(s - jnp.concatenate([m] * (width // 128), axis=1))
        total = fold(w, jnp.add)
        w = w * jnp.concatenate([1.0 / total] * (width // 128), axis=1)
        return w, m + jnp.log(total)

    def mix(t, w, g):
        mask = same(g.shape[0])
        pt = jnp.concatenate([jnp.where(mask, w[h:h + 1], 0.0).astype(BF16) for h in range(HEADS)], axis=0)
        ctx = jnp.dot(pt, g, preferred_element_type=F32)
        r0 = pl.multiple_of(t * TN, TN)
        for h in range(HEADS):
            cs[h, pl.ds(r0, TN), :] = ctx[h * TN:(h + 1) * TN].astype(BF16)

    gather(0, st0, edges)

    @pl.loop(0, tiles // 2)
    def _(i):
        t = 2 * i
        gather(t + 1, st1, edges)
        g0 = staged(st0, edges)
        s0 = scores(t, g0)
        gs[pl.ds(pl.multiple_of(t * edges, edges), edges), :] = g0
        gather(jnp.minimum(t + 2, tiles - 1), st0, edges)
        g1 = staged(st1, edges)
        s1 = scores(t + 1, g1)
        gs[pl.ds(pl.multiple_of((t + 1) * edges, edges), edges), :] = g1
        r0 = pl.multiple_of(i * 8, 8)
        ss[pl.ds(r0, 8), 0:edges] = jnp.concatenate([s0, s1], axis=0)

    w, lse = softmax(ss[:, 0:edges] + bias_ref[:, 0:edges])
    ss[:, 0:edges] = w
    lse_ref[...] = lse

    @pl.loop(0, tiles // 2)
    def _(i):
        both = ss[pl.ds(pl.multiple_of(i * 8, 8), 8), 0:edges]
        for j in range(2):
            t = 2 * i + j
            mix(t, both[4 * j:4 * j + 4], gs[pl.ds(pl.multiple_of(t * edges, edges), edges), :])

    if slots < K:

        def again(i, j):
            t = 2 * i + j
            full = K * TN
            gather(t, st0, full)
            g = staged(st0, full)
            rows8 = pl.ds(pl.multiple_of(i * 8, 8), 8)
            w, lse = softmax(scores(t, g) + bias_ref[rows8, :][4 * j:4 * j + 4])
            old = lse_ref[rows8, :]
            lse_ref[rows8, :] = jnp.concatenate([old[0:4], lse] if j else [lse, old[4:8]], axis=0)
            mix(t, w, g)

        @pl.loop(0, tiles // 2)
        def _(i):
            for j in range(2):
                pl.when(over_ref[2 * i + j] > 0)(functools.partial(again, i, j))

    for h in range(HEADS):
        s = slice(h * HEAD_DIM, (h + 1) * HEAD_DIM)
        wv = v_ref[h // 2, :, (h % 2) * HEAD_DIM:(h % 2 + 1) * HEAD_DIM]
        att_ref[:, s] = jnp.dot(cs[h], wv, preferred_element_type=F32).astype(BF16)


def attend(grid, idx, over, bias, mesh, w, v, *, slots, rows, side):
    nodes = mesh.shape[0]
    tiles = nodes // TN
    edges = slots * TN
    return pl.pallas_call(
        functools.partial(attend_kernel, tiles, slots, rows, side),
        out_shape=(jax.ShapeDtypeStruct((nodes, D), BF16), jax.ShapeDtypeStruct((tiles * HEADS, 128), F32)),
        in_specs=[ANY, SMEM, SMEM, VMEM, VMEM, VMEM, VMEM],
        out_specs=(VMEM, VMEM),
        scratch_shapes=[
            pltpu.VMEM((rows, D), BF16),
            pltpu.SemaphoreType.DMA((rows // CH,)),
            pltpu.VMEM((rows * 4, 128), F32),
            pltpu.VMEM((K * TN * 4, 128), F32),
            pltpu.VMEM((edges * 4, 128), F32),
            pltpu.VMEM((HEADS, nodes, D), BF16),
            pltpu.VMEM((HEADS, nodes, D), BF16),
            pltpu.VMEM((tiles * edges, D), BF16),
            pltpu.VMEM((tiles * HEADS, K * TN), F32),
        ],
        compiler_params=pltpu.CompilerParams(vmem_limit_bytes=56 * 1024 * 1024),
    )(grid, idx, over, bias, mesh, w, v)


def final_kernel(a0, a1, a2, l0, l1, l2, mesh_ref, wo_ref, gain_ref, keep_ref, send_ref, *, last):
    first = lax.axis_index("head") == 0
    lat = lax.axis_index("lat")
    has_low, has_high = lat > 0, lat < last
    has1 = jnp.where(first, has_high, has_low)
    has2 = jnp.where(first, has_low, has_high)
    nodes = mesh_ref.shape[0]
    tiles = nodes // TN
    x0 = l0[...]
    x1 = jnp.where(has1, l1[...], DEAD)
    rows = 4 * tiles
    order = lax.broadcasted_iota(jnp.int32, (rows, 128), 0) % 4
    swapped = jnp.where(order < 2, pltpu.roll(l2[...], rows - 2, 0), pltpu.roll(l2[...], 2, 0))
    x2 = jnp.where(has2, swapped, DEAD)
    top = jnp.maximum(x0, jnp.maximum(x1, x2))
    e = [jnp.exp(x - top) for x in (x0, x1, x2)]
    inv = 1.0 / (e[0] + e[1] + e[2])
    e = [x * inv for x in e]
    node = lax.broadcasted_iota(jnp.int32, (TN, 128), 0)
    lane = lax.broadcasted_iota(jnp.int32, (TN, 128), 1)
    mask = node == lane

    def column(i, h):
        parts = [
            jnp.sum(jnp.where(mask, e[i][t * 4 + h:t * 4 + h + 1, :], 0.0), axis=1, keepdims=True) for t in range(tiles)
        ]
        return jnp.concatenate(parts, axis=0)

    heads = []
    for h in range(HEADS):
        s = slice(h * HEAD_DIM, (h + 1) * HEAD_DIM)
        hx = (h + 2) % 4
        sx = slice(hx * HEAD_DIM, (hx + 1) * HEAD_DIM)
        mixed = (
            a0[:, s].astype(F32) * column(0, h)
            + a1[:, s].astype(F32) * column(1, h)
            + a2[:, sx].astype(F32) * column(2, h)
        )
        heads.append(mixed.astype(BF16))
    mine = jnp.concatenate(heads[0:2], axis=1)
    theirs = jnp.concatenate(heads[2:4], axis=1)
    projected = jnp.dot(mine, wo_ref[0], preferred_element_type=F32) + jnp.dot(
        theirs, wo_ref[1], preferred_element_type=F32
    )
    updated = mesh_ref[...].astype(F32) + projected
    mean = jnp.sum(updated, axis=1, keepdims=True) / D
    variance = jnp.sum(updated * updated, axis=1, keepdims=True) / D - mean * mean
    normed = (updated - mean) * lax.rsqrt(variance + EPSILON)
    left, right = normed[:, 0:256], normed[:, 256:512]
    keep_ref[...] = (jnp.where(first, left, right) * gain_ref[0:1, :]).astype(BF16)
    send_ref[...] = (jnp.where(first, right, left) * gain_ref[1:2, :]).astype(BF16)


def finish(own, r0, r1, mesh, wo, gain, last):
    nodes = mesh.shape[0]
    return pl.pallas_call(
        functools.partial(final_kernel, last=last),
        out_shape=(jax.ShapeDtypeStruct((nodes, D // 2), BF16),) * 2,
        in_specs=[VMEM] * 9,
        out_specs=(VMEM, VMEM),
    )(own[0], r0[0], r1[0], own[1], r0[1], r1[1], mesh, wo, gain)


def shards(
    grid_latent, mesh_latent, neighbours, edge_bias, query_weight, key_weight, value_weight, out_weight, norm_gain
):
    band = grid_latent.shape[0]
    count = mesh_latent.shape[0]
    half = count // 2
    lats = lax.axis_size("lat")
    c = lax.axis_index("head")
    offset = lax.axis_index("lat") * band
    both = ("lat", "head")

    def partner(x):
        return lax.ppermute(x, "head", [(0, 1), (1, 0)])

    def outward(cross):
        pairs = []
        for b in range(lats):
            if b + 1 < lats:
                pairs.append((2 * b + (1 if cross else 0), 2 * (b + 1)))
            if b > 0:
                pairs.append((2 * b + (0 if cross else 1), 2 * (b - 1) + 1))
        return pairs

    def homeward(cross):
        return [(target, source ^ (1 if cross else 0)) for source, target in outward(False)]

    def mine_of(x):
        return lax.dynamic_slice_in_dim(x, c * half, half, 0)

    def other_of(x):
        return lax.dynamic_slice_in_dim(x, (1 - c) * half, half, 0)

    mesh_c, mesh_o = mine_of(mesh_latent), other_of(mesh_latent)
    qa = lax.ppermute(mesh_c, both, outward(False))
    weights = jnp.concatenate([query_weight, key_weight], axis=1)
    weights = jnp.stack([weights, partner(weights)])
    values = jnp.stack([value_weight, partner(value_weight)])
    bias_o = partner(other_of(edge_bias))
    qb = lax.ppermute(mesh_o, both, outward(False))
    outs = jnp.stack([out_weight, partner(out_weight)])

    lanes = (count // 128, 128)
    nb_t = neighbours.T.reshape((K,) + lanes)
    bias_t = edge_bias.astype(F32).T.reshape((2 * K,) + lanes)
    idx, bias_same, bias_cross = compact(nb_t, bias_t, band)
    idx = lax.ppermute(idx, both, outward(False))
    bias_same = lax.ppermute(bias_same.astype(BF16), both, outward(False))
    bias_cross = lax.ppermute(bias_cross.astype(BF16), both, outward(True))

    tiles = half // TN
    nb_c = mine_of(neighbours) - offset
    inside = (nb_c >= 0) & (nb_c < band) & (mine_of(neighbours) >= 0)

    def tiled(x):
        return x.reshape(tiles, TN, K).transpose(0, 2, 1)

    own_idx = tiled(jnp.where(inside, nb_c * 4, 0)).reshape(-1)
    own_bias = jnp.concatenate([mine_of(edge_bias), bias_o], axis=1).astype(F32)
    own_bias = own_bias.reshape(tiles, TN, HEADS, K).transpose(0, 2, 3, 1)
    own_bias = jnp.where(tiled(inside)[:, None], own_bias, DEAD).reshape(tiles * HEADS, K * TN)
    none = jnp.zeros((tiles,), jnp.int32)
    own = attend(grid_latent, own_idx, none, own_bias, mesh_c, weights, values, slots=K, rows=band, side=0)

    idx = idx.reshape(K, 2 * tiles, TN).transpose(1, 0, 2)
    bias = jnp.concatenate([bias_same, bias_cross], axis=0).astype(F32).reshape(HEADS, K, 2 * tiles, TN)
    over = jnp.max(bias[0, 8], axis=1) > DEAD / 2
    bias = bias.transpose(2, 0, 1, 3)
    over = over.astype(jnp.int32)

    def visit(mesh, pick):
        return attend(
            grid_latent,
            pick(idx).reshape(-1),
            pick(over),
            pick(bias).reshape(tiles * HEADS, K * TN),
            mesh,
            weights,
            values,
            slots=8,
            rows=HALO,
            side=band - HALO,
        )

    def pick_mine(x):
        return lax.dynamic_slice_in_dim(x, c * tiles, tiles, 0)

    def pick_other(x):
        return lax.dynamic_slice_in_dim(x, (1 - c) * tiles, tiles, 0)

    na = visit(qa, pick_mine)
    r0 = [lax.ppermute(x, both, homeward(False)) for x in na]
    nb = visit(qb, pick_other)
    r1 = [lax.ppermute(x, both, homeward(True)) for x in nb]
    gain = norm_gain.astype(F32)[None]
    gain = jnp.concatenate([gain, partner(gain)], axis=0)
    keep, send = finish(own, r0, r1, mesh_c, outs, gain, lats - 1)
    got = partner(send)
    return jnp.where(c == 0, jnp.concatenate([keep, got], axis=0), jnp.concatenate([got, keep], axis=0))


def solution(mesh):
    in_specs = (
        P("lat", None),
        P("lat", None),
        P("lat", None),
        P("lat", "head"),
        P(None, "head"),
        P(None, "head"),
        P(None, "head"),
        P("head", None),
        P("head"),
    )
    out_specs = P("lat", "head")
    return jax.shard_map(shards, mesh=mesh, in_specs=in_specs, out_specs=out_specs, check_vma=False)
```

time: 210 us -> 122 us (0.58)
  the two profiles are of different devices: /device:TPU:97 before, /device:TPU:1 now
where the time goes in v1:
time: 122 us; the launch traced here: 121 us
  starting transfers between devices  50.9 us (42%)
  Pallas kernels  38.6 us (32%)
  local copies, waits for them, and re-layouts  17.6 us (14%)
  other arithmetic  11.5 us (9%)
  waiting for transfers between devices  2.23 us (2%)
    pallas_call x3, Pallas kernels, attend(): pl.pallas_call(functools.partial(attend_kernel, tiles, slots, rows, side)...  33 us
    ppermute x2, starting transfers between devices, shards(): r1 = [lax.ppermute(x, both, homeward(True)) for x in nb]  27.1 us
    ppermute x1, starting transfers between devices, shards(): bias_cross = lax.ppermute(bias_cross.astype(BF16), both, outward(True))  6.78 us
    ppermute x6, starting transfers between devices, partner(): return lax.ppermute(x, 'head', [(0, 1), (1, 0)])  6.21 us
    ppermute x2, starting transfers between devices, shards(): r0 = [lax.ppermute(x, both, homeward(False)) for x in na]  5.64 us
    pallas_call x1, Pallas kernels, finish(): pl.pallas_call(functools.partial(final_kernel, last=last), out_shape=(jax...  3.77 us
  transfers between devices with their start and end apart: 15, of which 2 were waited for; matrix products, arithmetic and copies ran while one was open for 19% of the time, Pallas kernels for 27%

profile of v1, /device:TPU:1, one launch (start us, length us, event | category | flops | bytes accessed | tf_op | source)
XLA Modules:
  0.0 121.1 jit_solution(2787065881961151097)
XLA Ops:
  1.5 1.4 %reshape.48.nb_ref = s32[16,5,128]{2,1,0:T(8,128)} reshape(s32[16,640]{1,0:T(8,128)} %bitcast.40) | data formatting | bytes 81920 | tf_op jit(solution)/shard_map/reshape | solution.py:326
  2.9 1.8 %shard_map.92 = (s32[16,5,128]{2,1,0:T(8,128)}, f32[32,5,128]{2,1,0:T(8,128)}, f32[32,5,128]{2,1,0:T(8,128)}) custom-call(s32[16,5,128]{2,1,0:T(8,128)} %reshape.48.nb_ref, f32[32,5,128]{2,1,0:T(8,128)} %reshape.57.bias_ref), custom_call_target="tpu_custom_call" | custom-call | tf_op jit(solution)/shard_map/pallas_call | solution.py:61
  4.6 0.9 convert_element_type.24
  5.5 1.3 %collective-permute-start.4 = (bf16[32,5,128]{2,1,0:T(8,128)(2,1)S(1)}, bf16[32,5,128]{2,1,0:T(8,128)(2,1)S(1)}, u32[]{:S(2)}, u32[]{:S(2)}) collective-permute-start(bf16[32,5,128]{2,1,0:T(8,128)(2,1)S(1)} %convert_element_type.24), channel_id=1, source_target_pairs={{0,2},{2,4},{3,1},{4,6},{5,3},{6,8},{7,5},{8,10},{9,7},{10,12},{11... | collective-permute-start | bytes 122888 | tf_op jit(solution)/shard_map/ppermute | solution.py:330
  6.8 0.9 convert_element_type.25
  7.8 6.8 %collective-permute-start.5 = (bf16[32,5,128]{2,1,0:T(8,128)(2,1)S(1)}, bf16[32,5,128]{2,1,0:T(8,128)(2,1)S(1)}, u32[]{:S(2)}, u32[]{:S(2)}) collective-permute-start(bf16[32,5,128]{2,1,0:T(8,128)(2,1)S(1)} %convert_element_type.25), channel_id=1, source_target_pairs={{1,2},{3,4},{2,1},{5,6},{4,3},{7,8},{6,5},{9,10},{8,7},{11,12},{10... | collective-permute-start | bytes 122888 | tf_op jit(solution)/shard_map/ppermute | solution.py:331
  14.6 1.3 %collective-permute-start.3 = (s32[16,5,128]{2,1,0:T(8,128)}, s32[16,5,128]{2,1,0:T(8,128)}, u32[]{:S(2)}, u32[]{:S(2)}) collective-permute-start(s32[16,5,128]{2,1,0:T(8,128)} %get-tuple-element.17), channel_id=1, source_target_pairs={{0,2},{2,4},{3,1},{4,6},{5,3},{6,8},{7,5},{8,10},{9,7},{10,12},{11... | collective-permute-start | bytes 122888 | tf_op jit(solution)/shard_map/ppermute | solution.py:329
  15.9 1.8 %constant_dynamic-slice_fusion = (bf16[320,512]{1,0:T(8,128)(2,1)}, bf16[320,512]{1,0:T(8,128)(2,1)S(1)}) fusion(bf16[640,512]{1,0:T(8,128)(2,1)} %param.10, s32[]{:T(128)S(6)} %select_n.39, s32[]{:T(128)S(6)} %select_n.37), kind=kLoop, calls=%fused_computation.17 | loop fusion | bytes 1310728 | tf_op jit(solution)/shard_map/dynamic_slice | solution.py:314
  17.7 1.3 %collective-permute-start.8 = (bf16[320,512]{1,0:T(8,128)(2,1)}, bf16[320,512]{1,0:T(8,128)(2,1)}, u32[]{:S(2)}, u32[]{:S(2)}) collective-permute-start(bf16[320,512]{1,0:T(8,128)(2,1)} %get-tuple-element.31), channel_id=1, source_target_pairs={{0,2},{2,4},{3,1},{4,6},{5,3},{6,8},{7,5},{8,10},{9,7},{10,12},{11... | collective-permute-start | bytes 983048 | tf_op jit(solution)/shard_map/ppermute | solution.py:322
  19.7 3.6 %collective-permute-start.13 = (f32[1,256]{1,0:T(1,128)S(1)}, f32[1,256]{1,0:T(1,128)S(1)}, u32[]{:S(2)}, u32[]{:S(2)}) collective-permute-start(f32[1,256]{1,0:T(1,128)S(1)} %bitcast.41), channel_id=1, source_target_pairs={{0,1},{1,0},{2,3},{3,2},{4,5},{5,4},{6,7},{7,6},{8,9},{9,8},{10,11... | collective-permute-start | bytes 3080 | tf_op jit(solution)/shard_map/ppermute | solution.py:296
  23.3 0.9 constant_dynamic-slice_fusion.3
  24.2 1.0 constant_dynamic-update-slice_fusion.1
  25.2 1.0 constant_dynamic-update-slice_fusion
  26.2 0.8 multiply_select_fusion
  30.5 1.3 %collective-permute-start.6 = (bf16[320,512]{1,0:T(8,128)(2,1)S(1)}, bf16[320,512]{1,0:T(8,128)(2,1)}, u32[]{:S(2)}, u32[]{:S(2)}) collective-permute-start(bf16[320,512]{1,0:T(8,128)(2,1)S(1)} %get-tuple-element.32.mesh_ref), channel_id=1, source_target_pairs={{0,2},{2,4},{3,1},{4,6},{5,3},{6,8},{7,5},{8,10},{9,7},{10,12},{11... | collective-permute-start | bytes 983048 | tf_op jit(solution)/shard_map/ppermute | solution.py:317
  33.2 2.0 %collective-permute-start.12 = (bf16[256,512]{1,0:T(8,128)(2,1)}, bf16[256,512]{1,0:T(8,128)(2,1)}, u32[]{:S(2)}, u32[]{:S(2)}) collective-permute-start(bf16[256,512]{1,0:T(8,128)(2,1)} %param.16), channel_id=1, source_target_pairs={{0,1},{1,0},{2,3},{3,2},{4,5},{5,4},{6,7},{7,6},{8,9},{9,8},{10,11... | collective-permute-start | bytes 786440 | tf_op jit(solution)/shard_map/ppermute | solution.py:296
  35.1 0.9 reshape.51
  37.6 0.8 reshape.53.bias_ref
  38.4 0.9 copy.16
  40.8 1.9 %pad_maximum_fusion.1.v_ref = bf16[2,512,256]{2,1,0:T(8,128)(2,1)} fusion(bf16[1,512,256]{2,1,0:T(8,128)(2,1)} %bitcast.6, bf16[1,512,256]{2,1,0:T(8,128)(2,1)} %bitcast.37), kind=kLoop, calls=%fused_computation.1 | loop fusion | flops 262144 | bytes 1048576 | tf_op jit(solution)/shard_map/stack | solution.py:320
  42.7 1.1 pad_maximum_fusion.w_ref
  43.8 9.1 %shard_map.94 = (bf16[320,512]{1,0:T(8,128)(2,1)}, f32[40,128]{1,0:T(8,128)}) custom-call(bf16[8192,512]{1,0:T(8,128)(2,1)} %grid_ref.5, s32[5120]{0:T(1024)} %reshape.54.idx_ref, s32[10]{0:T(128)} %get-tuple-element.37.over_ref, f32[40,512]{1,0:T(8,128)} %reshape.55.bias_ref, bf16[320,512]{1,0:T(8,128)(2,1)} %collective-permute-done.8.mesh_ref, ...), custom_call_target="tpu_custom_call" | custom-call | tf_op jit(solution)/shard_map/pallas_call | solution.py:201
  52.9 3.8 %collective-permute-start.9 = (bf16[320,512]{1,0:T(8,128)(2,1)}, bf16[320,512]{1,0:T(8,128)(2,1)S(1)}, u32[]{:S(2)}, u32[]{:S(2)}) collective-permute-start(bf16[320,512]{1,0:T(8,128)(2,1)} %get-tuple-element.21), channel_id=1, source_target_pairs={{2,1},{4,3},{1,2},{6,5},{3,4},{8,7},{5,6},{10,9},{7,8},{12,11},{9,... | collective-permute-start | bytes 983048 | tf_op jit(solution)/shard_map/ppermute | solution.py:376
  56.7 9.1 %shard_map.93 = (bf16[320,512]{1,0:T(8,128)(2,1)}, f32[40,128]{1,0:T(8,128)}) custom-call(bf16[8192,512]{1,0:T(8,128)(2,1)} %grid_ref.5, s32[5120]{0:T(1024)} %reshape.52.idx_ref, s32[10]{0:T(128)} %get-tuple-element.38.over_ref, f32[40,512]{1,0:T(8,128)} %reshape.53.bias_ref, bf16[320,512]{1,0:T(8,128)(2,1)} %collective-permute-done.6.mesh_ref, ...), custom_call_target="tpu_custom_call" | custom-call | tf_op jit(solution)/shard_map/pallas_call | solution.py:201
  65.8 4.2 %collective-permute-start.7 = (bf16[320,512]{1,0:T(8,128)(2,1)}, bf16[320,512]{1,0:T(8,128)(2,1)S(1)}, u32[]{:S(2)}, u32[]{:S(2)}) collective-permute-start(bf16[320,512]{1,0:T(8,128)(2,1)} %get-tuple-element.20), channel_id=1, source_target_pairs={{2,0},{4,2},{1,3},{6,4},{3,5},{8,6},{5,7},{10,8},{7,9},{12,10},{9,... | collective-permute-start | bytes 983048 | tf_op jit(solution)/shard_map/ppermute | solution.py:374
  70.9 23.3 %collective-permute-start.11 = (f32[40,128]{1,0:T(8,128)S(1)}, f32[40,128]{1,0:T(8,128)S(1)}, u32[]{:S(2)}, u32[]{:S(2)}) collective-permute-start(f32[40,128]{1,0:T(8,128)S(1)} %copy-done.7), channel_id=1, source_target_pairs={{2,1},{4,3},{1,2},{6,5},{3,4},{8,7},{5,6},{10,9},{7,8},{12,11},{9,... | collective-permute-start | bytes 61448 | tf_op jit(solution)/shard_map/ppermute | solution.py:376
  94.2 1.5 %collective-permute-start.10 = (f32[40,128]{1,0:T(8,128)}, f32[40,128]{1,0:T(8,128)S(1)}, u32[]{:S(2)}, u32[]{:S(2)}) collective-permute-start(f32[40,128]{1,0:T(8,128)} %get-tuple-element.23), channel_id=1, source_target_pairs={{2,0},{4,2},{1,3},{6,4},{3,5},{8,6},{5,7},{10,8},{7,9},{12,10},{9,... | collective-permute-start | bytes 61448 | tf_op jit(solution)/shard_map/ppermute | solution.py:374
  95.7 1.8 %pad_maximum_fusion.2.wo_ref = bf16[2,256,512]{2,1,0:T(8,128)(2,1)} fusion(bf16[1,256,512]{2,1,0:T(8,128)(2,1)} %bitcast.14, bf16[1,256,512]{2,1,0:T(8,128)(2,1)S(1)} %bitcast.38), kind=kLoop, calls=%fused_computation.2 | loop fusion | flops 262144 | bytes 1048576 | tf_op jit(solution)/shard_map/stack | solution.py:323
  98.1 14.8 %shard_map.91 = (bf16[320,512]{1,0:T(8,128)(2,1)}, f32[40,128]{1,0:T(8,128)}) custom-call(bf16[8192,512]{1,0:T(8,128)(2,1)} %grid_ref.5, s32[5120]{0:T(1024)} %reshape.45.idx_ref, s32[10]{0:T(128)} %broadcast_4_over_ref.2.over_ref, f32[40,512]{1,0:T(8,128)} %reshape.47.bias_ref, bf16[320,512]{1,0:T(8,128)(2,1)} %copy-done, ...), custom_call_target="tpu_custom_call" | custom-call | tf_op jit(solution)/shard_map/pallas_call | solution.py:201
  113.9 3.8 %shard_map.95 = (bf16[320,256]{1,0:T(8,128)(2,1)}, bf16[320,256]{1,0:T(8,128)(2,1)}) custom-call(bf16[320,512]{1,0:T(8,128)(2,1)} %get-tuple-element.16.a0, bf16[320,512]{1,0:T(8,128)(2,1)} %copy-done.2, bf16[320,512]{1,0:T(8,128)(2,1)} %copy-done.1, f32[40,128]{1,0:T(8,128)} %get-tuple-element.22.l0, f32[40,128]{1,0:T(8,128)} %copy-done.6, ...), custom_call_target="tpu_custom_call" | custom-call | tf_op jit(solution)/shard_map/pallas_call | solution.py:276
  117.7 1.6 %collective-permute-done.14 = bf16[320,256]{1,0:T(8,128)(2,1)S(1)} collective-permute-done((bf16[320,256]{1,0:T(8,128)(2,1)}, bf16[320,256]{1,0:T(8,128)(2,1)S(1)}, u32[]{:S(2)}, u32[]{:S(2)}) %collective-permute-start.14) | collective-permute-done | bytes 163872 | tf_op jit(solution)/shard_map/ppermute | solution.py:296
  119.3 1.8 %maximum_select_fusion = bf16[640,256]{1,0:T(8,128)(2,1)} fusion(bf16[320,256]{1,0:T(8,128)(2,1)S(1)} %collective-permute-done.14, bf16[320,256]{1,0:T(8,128)(2,1)} %get-tuple-element.25, pred[]{:T(512)S(6)} %eq.3), kind=kLoop, calls=%fused_computation.6 | loop fusion | flops 1474560 | bytes 655361 | tf_op jit(solution)/shard_map/jit(_where)/select_n | solution.py:381
  (61 shorter events, 12.3 us)
Async XLA Ops:
  5.5 24.5 %collective-permute-start.4 = (bf16[32,5,128]{2,1,0:T(8,128)(2,1)S(1)}, bf16[32,5,128]{2,1,0:T(8,128)(2,1)S(1)}, u32[]{:S(2)}, u32[]{:S(2)}) collective-permute-start(bf16[32,5,128]{2,1,0:T(8,128)(2,1)S(1)} %convert_element_type.24), channel_id=1, source_target_pairs={{0,2},{2,4},{3,1},{4,6},{5,3},{6,8},{7,5},{8,10},{9,7},{10,12},{11... | collective-permute-start | bytes 122888 | tf_op jit(solution)/shard_map/ppermute | solution.py:330
  7.8 22.7 %collective-permute-start.5 = (bf16[32,5,128]{2,1,0:T(8,128)(2,1)S(1)}, bf16[32,5,128]{2,1,0:T(8,128)(2,1)S(1)}, u32[]{:S(2)}, u32[]{:S(2)}) collective-permute-start(bf16[32,5,128]{2,1,0:T(8,128)(2,1)S(1)} %convert_element_type.25), channel_id=1, source_target_pairs={{1,2},{3,4},{2,1},{5,6},{4,3},{7,8},{6,5},{9,10},{8,7},{11,12},{10... | collective-permute-start | bytes 122888 | tf_op jit(solution)/shard_map/ppermute | solution.py:331
  14.6 18.6 %collective-permute-start.3 = (s32[16,5,128]{2,1,0:T(8,128)}, s32[16,5,128]{2,1,0:T(8,128)}, u32[]{:S(2)}, u32[]{:S(2)}) collective-permute-start(s32[16,5,128]{2,1,0:T(8,128)} %get-tuple-element.17), channel_id=1, source_target_pairs={{0,2},{2,4},{3,1},{4,6},{5,3},{6,8},{7,5},{8,10},{9,7},{10,12},{11... | collective-permute-start | bytes 122888 | tf_op jit(solution)/shard_map/ppermute | solution.py:329
  17.7 35.1 %copy-start = (bf16[320,512]{1,0:T(8,128)(2,1)}, bf16[320,512]{1,0:T(8,128)(2,1)S(1)}, u32[]{:S(2)}) copy-start(bf16[320,512]{1,0:T(8,128)(2,1)S(1)} %get-tuple-element.32.mesh_ref) | copy-start | bytes 983044
  17.7 26.0 %collective-permute-start.8 = (bf16[320,512]{1,0:T(8,128)(2,1)}, bf16[320,512]{1,0:T(8,128)(2,1)}, u32[]{:S(2)}, u32[]{:S(2)}) collective-permute-start(bf16[320,512]{1,0:T(8,128)(2,1)} %get-tuple-element.31), channel_id=1, source_target_pairs={{0,2},{2,4},{3,1},{4,6},{5,3},{6,8},{7,5},{8,10},{9,7},{10,12},{11... | collective-permute-start | bytes 983048 | tf_op jit(solution)/shard_map/ppermute | solution.py:322
  19.7 8.9 %collective-permute-start.13 = (f32[1,256]{1,0:T(1,128)S(1)}, f32[1,256]{1,0:T(1,128)S(1)}, u32[]{:S(2)}, u32[]{:S(2)}) collective-permute-start(f32[1,256]{1,0:T(1,128)S(1)} %bitcast.41), channel_id=1, source_target_pairs={{0,1},{1,0},{2,3},{3,2},{4,5},{5,4},{6,7},{7,6},{8,9},{9,8},{10,11... | collective-permute-start | bytes 3080 | tf_op jit(solution)/shard_map/ppermute | solution.py:296
  28.5 1.2 collective-permute-start
  29.7 12.9 %collective-permute-start.1 = (bf16[512,512]{1,0:T(8,128)(2,1)S(1)}, bf16[512,512]{1,0:T(8,128)(2,1)S(1)}, u32[]{:S(2)}, u32[]{:S(2)}) collective-permute-start(bf16[512,512]{1,0:T(8,128)(2,1)S(1)} %constant_dynamic-update-slice_fusion), channel_id=1, source_target_pairs={{0,1},{1,0},{2,3},{3,2},{4,5},{5,4},{6,7},{7,6},{8,9},{9,8},{10,11... | collective-permute-start | bytes 1572872 | tf_op jit(solution)/shard_map/ppermute | solution.py:296
  30.1 10.7 %collective-permute-start.2 = (bf16[512,256]{1,0:T(8,128)(2,1)}, bf16[512,256]{1,0:T(8,128)(2,1)}, u32[]{:S(2)}, u32[]{:S(2)}) collective-permute-start(bf16[512,256]{1,0:T(8,128)(2,1)} %param.15), channel_id=1, source_target_pairs={{0,1},{1,0},{2,3},{3,2},{4,5},{5,4},{6,7},{7,6},{8,9},{9,8},{10,11... | collective-permute-start | bytes 786440 | tf_op jit(solution)/shard_map/ppermute | solution.py:296
  30.5 26.2 %collective-permute-start.6 = (bf16[320,512]{1,0:T(8,128)(2,1)S(1)}, bf16[320,512]{1,0:T(8,128)(2,1)}, u32[]{:S(2)}, u32[]{:S(2)}) collective-permute-start(bf16[320,512]{1,0:T(8,128)(2,1)S(1)} %get-tuple-element.32.mesh_ref), channel_id=1, source_target_pairs={{0,2},{2,4},{3,1},{4,6},{5,3},{6,8},{7,5},{8,10},{9,7},{10,12},{11... | collective-permute-start | bytes 983048 | tf_op jit(solution)/shard_map/ppermute | solution.py:317
  33.2 62.6 %collective-permute-start.12 = (bf16[256,512]{1,0:T(8,128)(2,1)}, bf16[256,512]{1,0:T(8,128)(2,1)}, u32[]{:S(2)}, u32[]{:S(2)}) collective-permute-start(bf16[256,512]{1,0:T(8,128)(2,1)} %param.16), channel_id=1, source_target_pairs={{0,1},{1,0},{2,3},{3,2},{4,5},{5,4},{6,7},{7,6},{8,9},{9,8},{10,11... | collective-permute-start | bytes 786440 | tf_op jit(solution)/shard_map/ppermute | solution.py:296
  43.8 26.2 %copy-start.4 = (pred[10,32,16]{1,0,2:T(8,128)(4,1)S(1)}, pred[10,32,16]{1,0,2:T(8,128)(4,1)}, u32[]{:S(2)}) copy-start(pred[10,32,16]{1,0,2:T(8,128)(4,1)} %reshape.46) | copy-start | bytes 15364
  52.9 18.1 %copy-start.7 = (f32[40,128]{1,0:T(8,128)S(1)}, f32[40,128]{1,0:T(8,128)}, u32[]{:S(2)}) copy-start(f32[40,128]{1,0:T(8,128)} %get-tuple-element.24) | copy-start | bytes 61444
  52.9 42.9 %copy-start.3 = (bf16[256,512]{1,0:T(8,128)(2,1)S(1)}, bf16[256,512]{1,0:T(8,128)(2,1)}, u32[]{:S(2)}) copy-start(bf16[256,512]{1,0:T(8,128)(2,1)} %param.16) | copy-start | bytes 786436
  52.9 60.1 %collective-permute-start.9 = (bf16[320,512]{1,0:T(8,128)(2,1)}, bf16[320,512]{1,0:T(8,128)(2,1)S(1)}, u32[]{:S(2)}, u32[]{:S(2)}) collective-permute-start(bf16[320,512]{1,0:T(8,128)(2,1)} %get-tuple-element.21), channel_id=1, source_target_pairs={{2,1},{4,3},{1,2},{6,5},{3,4},{8,7},{5,6},{10,9},{7,8},{12,11},{9,... | collective-permute-start | bytes 983048 | tf_op jit(solution)/shard_map/ppermute | solution.py:376
  65.8 47.3 %collective-permute-start.7 = (bf16[320,512]{1,0:T(8,128)(2,1)}, bf16[320,512]{1,0:T(8,128)(2,1)S(1)}, u32[]{:S(2)}, u32[]{:S(2)}) collective-permute-start(bf16[320,512]{1,0:T(8,128)(2,1)} %get-tuple-element.20), channel_id=1, source_target_pairs={{2,0},{4,2},{1,3},{6,4},{3,5},{8,6},{5,7},{10,8},{7,9},{12,10},{9,... | collective-permute-start | bytes 983048 | tf_op jit(solution)/shard_map/ppermute | solution.py:374
  70.9 42.0 %collective-permute-start.11 = (f32[40,128]{1,0:T(8,128)S(1)}, f32[40,128]{1,0:T(8,128)S(1)}, u32[]{:S(2)}, u32[]{:S(2)}) collective-permute-start(f32[40,128]{1,0:T(8,128)S(1)} %copy-done.7), channel_id=1, source_target_pairs={{2,1},{4,3},{1,2},{6,5},{3,4},{8,7},{5,6},{10,9},{7,8},{12,11},{9,... | collective-permute-start | bytes 61448 | tf_op jit(solution)/shard_map/ppermute | solution.py:376
  94.2 18.7 %collective-permute-start.10 = (f32[40,128]{1,0:T(8,128)}, f32[40,128]{1,0:T(8,128)S(1)}, u32[]{:S(2)}, u32[]{:S(2)}) collective-permute-start(f32[40,128]{1,0:T(8,128)} %get-tuple-element.23), channel_id=1, source_target_pairs={{2,0},{4,2},{1,3},{6,4},{3,5},{8,6},{5,7},{10,8},{7,9},{12,10},{9,... | collective-permute-start | bytes 61448 | tf_op jit(solution)/shard_map/ppermute | solution.py:374
  113.0 0.6 copy-start.5
  113.0 0.6 copy-start.6
  113.0 0.7 copy-start.1
  113.0 0.8 copy-start.2
  117.7 1.6 %collective-permute-start.14 = (bf16[320,256]{1,0:T(8,128)(2,1)}, bf16[320,256]{1,0:T(8,128)(2,1)S(1)}, u32[]{:S(2)}, u32[]{:S(2)}) collective-permute-start(bf16[320,256]{1,0:T(8,128)(2,1)} %get-tuple-element.26), channel_id=1, source_target_pairs={{0,1},{1,0},{2,3},{3,2},{4,5},{5,4},{6,7},{7,6},{8,9},{9,8},{10,11... | collective-permute-start | bytes 491528 | tf_op jit(solution)/shard_map/ppermute | solution.py:296

commit v2 on v0

v2 whole, which is shorter than its diff:
```python
import functools

import jax
import jax.numpy as jnp
from jax import lax
from jax.experimental import pallas as pl
from jax.experimental.pallas import tpu as pltpu
from jax.sharding import PartitionSpec as P

D = 512
K = 16
HEADS = 4
HEAD_DIM = 128
HALO = 2048
EPSILON = 1e-05
TN = 32
EDGES = K * TN
CH = 512
PIECE = 256
DEAD = -1e30
VMEM = pl.BlockSpec(memory_space=pltpu.VMEM)
SMEM = pl.BlockSpec(memory_space=pltpu.SMEM)
ANY = pl.BlockSpec(memory_space=pl.ANY)
MESH = pl.DeviceIdType.MESH
NT = (((1,), (1,)), ((), ()))
F32 = jnp.float32
BF16 = jnp.bfloat16


def kernel(
    last, grid_ref, idx_ref, bias_ref, mesh_ref, wq_ref, wk_ref, wv_ref, wo_ref, gain_ref, out_ref,
    buf, hbuf, table, st0, st1, qs, cs, gs, ss, wq2, wk2, wv2, wo2, gain2, bias2, out_send, out_recv,
    load_sem, ici_send, ici_recv, fwd_send, fwd_recv, w_send, w_recv, x_send, x_recv,
):
    band = grid_ref.shape[0]
    half = mesh_ref.shape[0] // 2
    tiles = half // TN
    share = HALO // 2
    pieces = share // PIECE
    lat = lax.axis_index("lat")
    c = lax.axis_index("head")
    other = 1 - c
    has_low, has_high = lat > 0, lat < last
    below, above = jnp.maximum(lat - 1, 0), jnp.minimum(lat + 1, last)

    chunks = band // CH
    loads = [
        pltpu.make_async_copy(grid_ref.at[pl.ds(i * CH, CH), :], buf.at[pl.ds(i * CH, CH), :], load_sem.at[i])
        for i in range(chunks)
    ]
    for load in loads:
        load.start()

    barrier = pltpu.get_barrier_semaphore()
    pl.semaphore_signal(barrier, inc=1, device_id=(lat, other), device_id_type=MESH)

    @pl.when(has_low)
    def _():
        pl.semaphore_signal(barrier, inc=1, device_id=(below, c), device_id_type=MESH)

    @pl.when(has_high)
    def _():
        pl.semaphore_signal(barrier, inc=1, device_id=(above, c), device_id_type=MESH)

    pl.semaphore_wait(barrier, 1 + has_low.astype(jnp.int32) + has_high.astype(jnp.int32))

    def crossing(side, i):
        start = band - HALO if side == 0 else 0
        rows = pl.ds(pl.multiple_of(start + c * share + i * PIECE, PIECE), PIECE)
        return pltpu.make_async_remote_copy(
            src_ref=grid_ref.at[rows, :],
            dst_ref=hbuf.at[side, 0, pl.ds(i * PIECE, PIECE), :],
            send_sem=ici_send.at[side, i],
            recv_sem=ici_recv.at[side, i],
            device_id=(above if side == 0 else below, c),
            device_id_type=MESH,
        )

    def forward(side, i):
        return pltpu.make_async_remote_copy(
            src_ref=hbuf.at[side, 0, pl.ds(i * PIECE, PIECE), :],
            dst_ref=hbuf.at[side, 1, pl.ds(i * PIECE, PIECE), :],
            send_sem=fwd_send.at[side, i],
            recv_sem=fwd_recv.at[side, i],
            device_id=(lat, other),
            device_id_type=MESH,
        )

    for i in range(pieces):

        @pl.when(has_high)
        def _():
            crossing(0, i).start()

        @pl.when(has_low)
        def _():
            crossing(1, i).start()

    pairs = tiles // 2
    given = [
        (wq_ref, wq2),
        (wk_ref, wk2),
        (bias_ref.at[pl.ds(other * pairs, pairs)], bias2),
        (wv_ref, wv2),
        (wo_ref, wo2),
        (gain_ref, gain2),
    ]
    gifts = [
        pltpu.make_async_remote_copy(
            src_ref=source,
            dst_ref=target,
            send_sem=w_send.at[i],
            recv_sem=w_recv.at[i],
            device_id=(lat, other),
            device_id_type=MESH,
        )
        for i, (source, target) in enumerate(given)
    ]
    for gift in gifts:
        gift.start()

    mesh_rows = mesh_ref[pl.ds(pl.multiple_of(c * half, half), half), :]

    def absorbed(part, wq, wk):
        q = jnp.dot(mesh_rows, wq[...], preferred_element_type=F32).astype(BF16)
        for j in range(2):
            s = slice(j * HEAD_DIM, (j + 1) * HEAD_DIM)
            qk = lax.dot_general(q[:, s], wk[:, s], NT, preferred_element_type=F32)
            qs[2 * part + j] = (qk * HEAD_DIM ** -0.5).astype(BF16)

    flat = table.reshape(table.shape[0] * 4, 128)

    def convert(rows, at, count):
        for col in range(4):
            flat[pl.ds(at * 4 + col, count, stride=4), :] = rows[:, col * 128:(col + 1) * 128].astype(F32)

    absorbed(0, wq_ref, wk_ref)
    for i in range(chunks):
        loads[i].wait()
        convert(buf.at[pl.ds(i * CH, CH), :], HALO + i * CH, CH)
    for gift in gifts:
        gift.wait()
    absorbed(1, wq2, wk2)

    side_rows = (0, HALO + band)

    def arrive(side, i):
        crossing(side, i).wait_recv()
        forward(side, i).start()
        convert(hbuf.at[side, 0, pl.ds(i * PIECE, PIECE), :], side_rows[side] + i * PIECE, PIECE)

    def arrive_forwarded(side, i):
        forward(side, i).wait()
        convert(hbuf.at[side, 1, pl.ds(i * PIECE, PIECE), :], side_rows[side] + share + i * PIECE, PIECE)

    for i in range(pieces + 1):
        for side, has in ((0, has_low), (1, has_high)):
            if i < pieces:
                pl.when(has)(functools.partial(arrive, side, i))
        for side, has in ((0, has_low), (1, has_high)):
            if i > 0:
                pl.when(has)(functools.partial(arrive_forwarded, side, i - 1))

    first_edge = c * (tiles * EDGES)
    node = lax.broadcasted_iota(jnp.int32, (TN, EDGES), 0)
    lane = lax.broadcasted_iota(jnp.int32, (TN, EDGES), 1)
    same = (lane % TN) == node

    def gather(t, st):
        for p in range(EDGES):
            st[p] = table[idx_ref[first_edge + t * EDGES + p]]

    def scores(t, st):
        st = st.reshape(EDGES * 4, 128)
        g = jnp.concatenate([st[pl.ds(col, EDGES, stride=4), :].astype(BF16) for col in range(4)], axis=1)
        gs[pl.ds(pl.multiple_of(t * EDGES, EDGES), EDGES), :] = g
        r0 = pl.multiple_of(t * TN, TN)
        qt = jnp.concatenate([qs[h, pl.ds(r0, TN), :] for h in range(HEADS)], axis=0)
        sc = lax.dot_general(qt, g, NT, preferred_element_type=F32)
        return [jnp.sum(jnp.where(same, sc[h * TN:(h + 1) * TN], 0.0), axis=0, keepdims=True) for h in range(HEADS)]

    gather(0, st0)

    @pl.loop(0, pairs)
    def _(i):
        t = 2 * i
        gather(t + 1, st1)
        s0 = scores(t, st0)
        gather(jnp.minimum(t + 2, tiles - 1), st0)
        s1 = scores(t + 1, st1)
        ss[i] = jnp.concatenate(s0[0:2] + s1[0:2] + s0[2:4] + s1[2:4], axis=0)

    blocks = EDGES // 128

    def fold(x, op):
        y = x[..., 0:128]
        for j in range(1, blocks):
            y = op(y, x[..., j * 128:(j + 1) * 128])
        y = op(y, pltpu.roll(y, 64, y.ndim - 1))
        return op(y, pltpu.roll(y, 32, y.ndim - 1))

    mine = bias_ref[pl.ds(c * pairs, pairs)]
    bias = jnp.concatenate([mine, bias2[...]], axis=1)
    s = ss[...] + bias
    m = fold(s, jnp.maximum)
    w = jnp.exp(s - jnp.concatenate([m] * blocks, axis=2))
    total = fold(w, jnp.add)
    ss[...] = w * jnp.concatenate([1.0 / total] * blocks, axis=2)

    @pl.loop(0, pairs)
    def _(i):
        both = ss[i]
        for j in range(2):
            t = 2 * i + j
            rows = [both[part * 4 + j * 2 + h:part * 4 + j * 2 + h + 1] for part in range(2) for h in range(2)]
            pt = jnp.concatenate([jnp.where(same, row, 0.0).astype(BF16) for row in rows], axis=0)
            g = gs[pl.ds(pl.multiple_of(t * EDGES, EDGES), EDGES), :]
            ctx = jnp.dot(pt, g, preferred_element_type=F32)
            r0 = pl.multiple_of(t * TN, TN)
            for h in range(HEADS):
                cs[h, pl.ds(r0, TN), :] = ctx[h * TN:(h + 1) * TN].astype(BF16)

    projected = jnp.zeros((half, D), F32)
    for part, (wv, wo) in enumerate(((wv_ref, wo_ref), (wv2, wo2))):
        attended = [
            jnp.dot(cs[2 * part + j], wv[:, j * HEAD_DIM:(j + 1) * HEAD_DIM], preferred_element_type=F32).astype(BF16)
            for j in range(2)
        ]
        projected = projected + jnp.dot(jnp.concatenate(attended, axis=1), wo[...], preferred_element_type=F32)
    updated = mesh_ref[pl.ds(pl.multiple_of(c * half, half), half), :].astype(F32) + projected
    mean = jnp.sum(updated, axis=1, keepdims=True) / D
    variance = jnp.sum(updated * updated, axis=1, keepdims=True) / D - mean * mean
    normed = (updated - mean) * lax.rsqrt(variance + EPSILON)
    left, right = normed[:, 0:D // 2], normed[:, D // 2:D]
    first = c == 0
    out_send[...] = (jnp.where(first, right, left) * gain2[0:1, :]).astype(BF16)
    swap = pltpu.make_async_remote_copy(
        src_ref=out_send,
        dst_ref=out_recv,
        send_sem=x_send,
        recv_sem=x_recv,
        device_id=(lat, other),
        device_id_type=MESH,
    )
    out_ref[pl.ds(pl.multiple_of(c * half, half), half), :] = (
        jnp.where(first, left, right) * gain_ref[0:1, :]
    ).astype(BF16)
    swap.start()
    swap.wait()
    out_ref[pl.ds(pl.multiple_of(other * half, half), half), :] = out_recv[...]
    for side, has in ((0, has_high), (1, has_low)):
        for i in range(pieces):

            @pl.when(has)
            def _():
                crossing(side, i).wait_send()


def shards(
    grid_latent, mesh_latent, neighbours, edge_bias, query_weight, key_weight, value_weight, out_weight, norm_gain
):
    band = grid_latent.shape[0]
    count = mesh_latent.shape[0]
    half = count // 2
    tiles = half // TN
    pieces = HALO // 2 // PIECE
    width = D // 2
    c = lax.axis_index("head")
    local = neighbours - (lax.axis_index("lat") * band - HALO)
    halo = (local < HALO) | (local >= HALO + band)
    row = jnp.where(halo, local ^ (c * (HALO // 2)), local)
    row = jnp.where(neighbours >= 0, row, HALO)
    idx = row.reshape(2 * tiles, TN, K).transpose(0, 2, 1).reshape(-1)
    live = (neighbours >= 0)[:, None, :]
    bias = jnp.where(live, edge_bias.astype(F32).reshape(count, 2, K), DEAD)
    bias = bias.reshape(tiles, 2, TN, 2, K).transpose(0, 1, 3, 4, 2).reshape(tiles, 4, EDGES)
    gain = jnp.broadcast_to(norm_gain.astype(F32)[None], (8, width))
    dma = pltpu.SemaphoreType.DMA
    out = pl.pallas_call(
        functools.partial(kernel, lax.axis_size("lat") - 1),
        out_shape=jax.ShapeDtypeStruct((count, width), BF16),
        in_specs=[ANY, SMEM] + [VMEM] * 7,
        out_specs=VMEM,
        scratch_shapes=[
            pltpu.VMEM((band, D), BF16),
            pltpu.VMEM((2, 2, HALO // 2, D), BF16),
            pltpu.VMEM((band + 2 * HALO, 4, 128), F32),
            pltpu.VMEM((EDGES, 4, 128), F32),
            pltpu.VMEM((EDGES, 4, 128), F32),
            pltpu.VMEM((HEADS, half, D), BF16),
            pltpu.VMEM((HEADS, half, D), BF16),
            pltpu.VMEM((tiles * EDGES, D), BF16),
            pltpu.VMEM((tiles // 2, 8, EDGES), F32),
            pltpu.VMEM((D, width), BF16),
            pltpu.VMEM((D, width), BF16),
            pltpu.VMEM((D, width), BF16),
            pltpu.VMEM((width, D), BF16),
            pltpu.VMEM((8, width), F32),
            pltpu.VMEM((tiles // 2, 4, EDGES), F32),
            pltpu.VMEM((half, width), BF16),
            pltpu.VMEM((half, width), BF16),
            dma((band // CH,)),
            dma((2, pieces)),
            dma((2, pieces)),
            dma((2, pieces)),
            dma((2, pieces)),
            dma((6,)),
            dma((6,)),
            dma,
            dma,
        ],
        compiler_params=pltpu.CompilerParams(
            collective_id=0, has_side_effects=True, vmem_limit_bytes=60 * 1024 * 1024
        ),
    )(grid_latent, idx, bias, mesh_latent, query_weight, key_weight, value_weight, out_weight, gain)
    return out


def solution(mesh):
    in_specs = (
        P("lat", None),
        P("lat", None),
        P("lat", None),
        P("lat", "head"),
        P(None, "head"),
        P(None, "head"),
        P(None, "head"),
        P("head", None),
        P("head"),
    )
    out_specs = P("lat", "head")
    return jax.shard_map(shards, mesh=mesh, in_specs=in_specs, out_specs=out_specs, check_vma=False)
```

time: 210 us -> 53.8 us (0.26); the launches traced: 207 us -> 53.4 us
  local copies, waits for them, and re-layouts: 113 us -> 5.87 us
  other arithmetic: 49 us -> 1.63 us
  Pallas kernels: 0 us -> 45.9 us
  starting transfers between devices: 19.1 us -> 0 us
  matrix products: 13.2 us -> 0 us
  blocking collectives: 7.63 us -> 0 us
  waiting for transfers between devices: 4.72 us -> 0 us
    gather x2 -> x0, local copies, waits for them, and re-layouts: 84.3 us -> none  [the longest x1 42.2 us: partial_softmax(): jnp.take(values, safe_rows, axis=0).reshape(count, K, local_heads, HEAD_DIM)]
    pallas_call x0 -> x1, Pallas kernels: none -> 45.9 us  [shards(): pl.pallas_call(functools.partial(kernel, lax.axis_size('lat') - 1), out_s...]
    concatenate x2 -> x0, other arithmetic: 20.6 us -> none  [extended(): block = jnp.concatenate([low, block, high], axis=dim)]
    ppermute x4 -> x0, starting transfers between devices: 19.1 us -> none  [the longest x2 14 us: extended(): lax.ppermute(lax.slice_in_dim(block, 0, width, axis=dim), axis, backward)]
    unnamed x1 -> x0, other arithmetic: 15.3 us -> none
    reshape x3 -> x4, local copies, waits for them, and re-layouts: 17 us -> 2.7 us  [the longest x1 1.08 us: shards(): bias = jnp.where(live, edge_bias.astype(F32).reshape(count, 2, K), DEAD)]
    dot_general x5 -> x0, matrix products: 13.2 us -> none  [the longest x1 6.11 us: shards(): jnp.dot(grid_latent, key_weight, preferred_element_type=jnp.float32)]
    select_n x2 -> x1, other arithmetic: 10.6 us -> 0.79 us  [shards(): row = jnp.where(neighbours >= 0, row, HALO)]
  transfers between devices with their start and end apart: 4 -> 0, of which waited for: 2 -> 0; matrix products, arithmetic and copies ran while one was open for 27% -> 0% of each run, Pallas kernels for 0% -> 0%
where the time goes in v2:
time: 53.8 us; the launch traced here: 53.4 us
  Pallas kernels  45.9 us (85%)
  local copies, waits for them, and re-layouts  5.87 us (11%)
  other arithmetic  1.63 us (3%)
    pallas_call x1, Pallas kernels, shards(): pl.pallas_call(functools.partial(kernel, lax.axis_size('lat') - 1), out_s...  45.9 us
    unnamed x1, local copies, waits for them, and re-layouts  1.72 us
    broadcast_in_dim x1, local copies, waits for them, and re-layouts, shards(): gain = jnp.broadcast_to(norm_gain.astype(F32)[None], (8, width))  1.25 us
    reshape x1, local copies, waits for them, and re-layouts, shards(): bias = jnp.where(live, edge_bias.astype(F32).reshape(count, 2, K), DEAD)  1.08 us

profile of v2, /device:TPU:97, one launch (start us, length us, event | category | flops | bytes accessed | tf_op | source)
XLA Modules:
  0.0 53.4 jit_solution(10688086345844900144)
XLA Ops:
  0.0 0.8 %fusion.1 = s32[640,16]{0,1:T(8,128)S(1)} fusion(s32[640,16]{0,1:T(8,128)} %param.11, s32[]{:T(128)S(6)} %mul.7, s32[]{:T(128)S(6)} %sub.9), kind=kLoop, calls=%fused_computation.3 | loop fusion | flops 81920 | bytes 81928 | tf_op jit(solution)/shard_map/jit(_where)/select_n | solution.py:272
  0.8 0.1 reshape.21
  0.9 0.7 %reshape.22.idx_ref = s32[10240]{0:T(1024)} reshape(s32[20,16,32]{2,1,0:T(8,128)S(1)} %copy.12) | data formatting | bytes 81920 | tf_op jit(solution)/shard_map/reshape | solution.py:273
  1.7 1.1 %reshape.27 = f32[10,2,32,2,16]{2,1,0,4,3:T(2,128)S(1)} reshape(bf16[640,32]{0,1:T(8,128)(2,1)} %param.12) | data formatting | bytes 122880 | tf_op jit(solution)/shard_map/reshape | solution.py:275
  2.7 0.8 %broadcast_compare_fusion = pred[640,16]{0,1:T(8,128)(4,1)S(1)} fusion(s32[640,16]{0,1:T(8,128)} %param.11), kind=kLoop, calls=%fused_computation.4 | loop fusion | flops 10240 | bytes 51200 | tf_op jit(solution)/shard_map/ge | solution.py:272
  3.5 0.1 broadcast_in_dim.23
  3.8 0.8 %reshape.25.bias_ref = f32[10,4,512]{2,1,0:T(4,128)} reshape(f32[10,2,2,16,32]{4,3,2,1,0:T(8,128)S(1)} %fusion) | data formatting | bytes 163840 | tf_op jit(solution)/shard_map/reshape | solution.py:276
  4.6 1.3 %broadcast_in_dim.26.gain_ref = f32[8,256]{1,0:T(8,128)} broadcast(bf16[256]{0:T(256)(128)(2,1)} %param.17), dimensions={1} | broadcast | bytes 8704 | tf_op jit(solution)/shard_map/broadcast_in_dim | solution.py:277
  5.8 45.9 %shard_map.91 = bf16[640,256]{1,0:T(8,128)(2,1)} custom-call(bf16[8192,512]{1,0:T(8,128)(2,1)} %grid_ref.1, s32[10240]{0:T(1024)} %reshape.22.idx_ref, f32[10,4,512]{2,1,0:T(4,128)} %reshape.25.bias_ref, bf16[640,512]{1,0:T(8,128)(2,1)} %mesh_ref.1, bf16[512,256]{1,0:T(8,128)(2,1)} %wq_ref.1, bf16[512,256]{1,0:T(8,128)(2,1)} %wk_ref.1, ...), custom_call_target="tpu_custom_call" | custom-call | tf_op jit(solution)/shard_map/pallas_call | solution.py:279
  51.7 1.7 %copy.19 = bf16[640,256]{1,0:T(8,128)(2,1)} copy(bf16[640,256]{1,0:T(8,128)(2,1)} %shard_map.91) | data formatting | bytes 655360
  (3 shorter events, 0.1 us)

commit v3 on v2

--- a/solution.py
+++ b/solution.py
@@ -28,9 +28,10 @@
 
 
 def kernel(
-    last, grid_ref, idx_ref, bias_ref, mesh_ref, wq_ref, wk_ref, wv_ref, wo_ref, gain_ref, out_ref,
+    last, grid_ref, nb_ref, bias_ref, mesh_ref, wq_ref, wk_ref, wv_ref, wo_ref, gain_ref, out_ref,
     buf, hbuf, table, st0, st1, qs, cs, gs, ss, wq2, wk2, wv2, wo2, gain2, bias2, out_send, out_recv,
-    load_sem, ici_send, ici_recv, fwd_send, fwd_recv, w_send, w_recv, x_send, x_recv,
+    channels, spread, rows_v, load_sem, ici_send, ici_recv, fwd_send, fwd_recv, w_send, w_recv, x_send, x_recv, s_sem,
+    *row_refs,
 ):
     band = grid_ref.shape[0]
     half = mesh_ref.shape[0] // 2
@@ -100,7 +101,7 @@
     given = [
         (wq_ref, wq2),
         (wk_ref, wk2),
-        (bias_ref.at[pl.ds(other * pairs, pairs)], bias2),
+        (bias_ref, bias2),
         (wv_ref, wv2),
         (wo_ref, wo2),
         (gain_ref, gain2),
@@ -142,6 +143,44 @@
         gift.wait()
     absorbed(1, wq2, wk2)
 
+    node = lax.broadcasted_iota(jnp.int32, (TN, EDGES), 0)
+    lane = lax.broadcasted_iota(jnp.int32, (TN, EDGES), 1)
+    same = (lane % TN) == node
+
+    nb = nb_ref[...]
+    local = nb - (lat * band - HALO)
+    live = nb >= 0
+    at_end = (local < HALO) | (local >= HALO + band)
+    row = jnp.where(live, jnp.where(at_end, local ^ (c * share), local), HALO)
+    row = jnp.clip(row, 0, band + 2 * HALO - 1)
+    stack = []
+    for values in (bias_ref[...].astype(F32), bias2[...].astype(F32)):
+        stack += [jnp.where(live, values[j * K:(j + 1) * K, :], DEAD) for j in range(2)]
+    stack += [(row >> 6).astype(F32), (row & 63).astype(F32)]
+    channels[...] = jnp.concatenate(stack, axis=0).T
+    slot = lax.broadcasted_iota(jnp.int32, (K, EDGES), 0)
+    slot_lane = lax.broadcasted_iota(jnp.int32, (K, EDGES), 1)
+    place = jnp.where(slot_lane // TN == slot, 1.0, 0.0).astype(BF16)
+
+    @pl.loop(0, pairs)
+    def _(i):
+        lines = []
+        for j in range(2):
+            r0 = pl.multiple_of(c * half + (2 * i + j) * TN, TN)
+            mixed = channels[pl.ds(r0, TN), :]
+            parts = jnp.concatenate([mixed[:, n * K:(n + 1) * K] for n in range(6)], axis=0).astype(BF16)
+            wide = jnp.dot(parts, place, preferred_element_type=F32)
+            line = [
+                jnp.sum(jnp.where(same, wide[n * TN:(n + 1) * TN], 0.0), axis=0, keepdims=True) for n in range(6)
+            ]
+            rows_v[2 * i + j] = jnp.clip((line[4] * 64.0 + line[5]).astype(jnp.int32), 0, band + 2 * HALO - 1) * 4
+            lines.append(line)
+        spread[i] = jnp.concatenate(lines[0][0:2] + lines[1][0:2] + lines[0][2:4] + lines[1][2:4], axis=0)
+
+    fetches = [pltpu.make_async_copy(rows_v.at[t], row_refs[t], s_sem.at[t]) for t in range(tiles)]
+    for fetch in fetches:
+        fetch.start()
+
     side_rows = (0, HALO + band)
 
     def arrive(side, i):
@@ -161,34 +200,31 @@
             if i > 0:
                 pl.when(has)(functools.partial(arrive_forwarded, side, i - 1))
 
-    first_edge = c * (tiles * EDGES)
-    node = lax.broadcasted_iota(jnp.int32, (TN, EDGES), 0)
-    lane = lax.broadcasted_iota(jnp.int32, (TN, EDGES), 1)
-    same = (lane % TN) == node
+    for fetch in fetches:
+        fetch.wait()
 
     def gather(t, st):
         for p in range(EDGES):
-            st[p] = table[idx_ref[first_edge + t * EDGES + p]]
+            st[p] = flat[pl.ds(row_refs[t][0, p], 4), :]
 
     def scores(t, st):
         st = st.reshape(EDGES * 4, 128)
         g = jnp.concatenate([st[pl.ds(col, EDGES, stride=4), :].astype(BF16) for col in range(4)], axis=1)
-        gs[pl.ds(pl.multiple_of(t * EDGES, EDGES), EDGES), :] = g
-        r0 = pl.multiple_of(t * TN, TN)
-        qt = jnp.concatenate([qs[h, pl.ds(r0, TN), :] for h in range(HEADS)], axis=0)
+        gs[t * EDGES:(t + 1) * EDGES, :] = g
+        qt = jnp.concatenate([qs[h, t * TN:(t + 1) * TN, :] for h in range(HEADS)], axis=0)
         sc = lax.dot_general(qt, g, NT, preferred_element_type=F32)
         return [jnp.sum(jnp.where(same, sc[h * TN:(h + 1) * TN], 0.0), axis=0, keepdims=True) for h in range(HEADS)]
 
+    stages = (st0, st1)
     gather(0, st0)
-
-    @pl.loop(0, pairs)
-    def _(i):
-        t = 2 * i
-        gather(t + 1, st1)
-        s0 = scores(t, st0)
-        gather(jnp.minimum(t + 2, tiles - 1), st0)
-        s1 = scores(t + 1, st1)
-        ss[i] = jnp.concatenate(s0[0:2] + s1[0:2] + s0[2:4] + s1[2:4], axis=0)
+    lines = []
+    for t in range(tiles):
+        if t + 1 < tiles:
+            gather(t + 1, stages[(t + 1) % 2])
+        lines.append(scores(t, stages[t % 2]))
+        if t % 2:
+            s0, s1 = lines[t - 1], lines[t]
+            ss[t // 2] = jnp.concatenate(s0[0:2] + s1[0:2] + s0[2:4] + s1[2:4], axis=0)
 
     blocks = EDGES // 128
 
@@ -199,9 +235,7 @@
         y = op(y, pltpu.roll(y, 64, y.ndim - 1))
         return op(y, pltpu.roll(y, 32, y.ndim - 1))
 
-    mine = bias_ref[pl.ds(c * pairs, pairs)]
-    bias = jnp.concatenate([mine, bias2[...]], axis=1)
-    s = ss[...] + bias
+    s = ss[...] + spread[...]
     m = fold(s, jnp.maximum)
     w = jnp.exp(s - jnp.concatenate([m] * blocks, axis=2))
     total = fold(w, jnp.add)
@@ -233,7 +267,7 @@
     normed = (updated - mean) * lax.rsqrt(variance + EPSILON)
     left, right = normed[:, 0:D // 2], normed[:, D // 2:D]
     first = c == 0
-    out_send[...] = (jnp.where(first, right, left) * gain2[0:1, :]).astype(BF16)
+    out_send[...] = (jnp.where(first, right, left) * gain2[...].astype(F32)).astype(BF16)
     swap = pltpu.make_async_remote_copy(
         src_ref=out_send,
         dst_ref=out_recv,
@@ -243,11 +277,11 @@
         device_id_type=MESH,
     )
     out_ref[pl.ds(pl.multiple_of(c * half, half), half), :] = (
-        jnp.where(first, left, right) * gain_ref[0:1, :]
-    ).astype(BF16)
+        jnp.where(first, left, right) * gain_ref[...].astype(F32)
+    )
     swap.start()
     swap.wait()
-    out_ref[pl.ds(pl.multiple_of(other * half, half), half), :] = out_recv[...]
+    out_ref[pl.ds(pl.multiple_of(other * half, half), half), :] = out_recv[...].astype(F32)
     for side, has in ((0, has_high), (1, has_low)):
         for i in range(pieces):
 
@@ -265,21 +299,11 @@
     tiles = half // TN
     pieces = HALO // 2 // PIECE
     width = D // 2
-    c = lax.axis_index("head")
-    local = neighbours - (lax.axis_index("lat") * band - HALO)
-    halo = (local < HALO) | (local >= HALO + band)
-    row = jnp.where(halo, local ^ (c * (HALO // 2)), local)
-    row = jnp.where(neighbours >= 0, row, HALO)
-    idx = row.reshape(2 * tiles, TN, K).transpose(0, 2, 1).reshape(-1)
-    live = (neighbours >= 0)[:, None, :]
-    bias = jnp.where(live, edge_bias.astype(F32).reshape(count, 2, K), DEAD)
-    bias = bias.reshape(tiles, 2, TN, 2, K).transpose(0, 1, 3, 4, 2).reshape(tiles, 4, EDGES)
-    gain = jnp.broadcast_to(norm_gain.astype(F32)[None], (8, width))
     dma = pltpu.SemaphoreType.DMA
     out = pl.pallas_call(
         functools.partial(kernel, lax.axis_size("lat") - 1),
-        out_shape=jax.ShapeDtypeStruct((count, width), BF16),
-        in_specs=[ANY, SMEM] + [VMEM] * 7,
+        out_shape=jax.ShapeDtypeStruct((count, width), F32),
+        in_specs=[ANY] + [VMEM] * 8,
         out_specs=VMEM,
         scratch_shapes=[
             pltpu.VMEM((band, D), BF16),
@@ -295,10 +319,13 @@
             pltpu.VMEM((D, width), BF16),
             pltpu.VMEM((D, width), BF16),
             pltpu.VMEM((width, D), BF16),
-            pltpu.VMEM((8, width), F32),
-            pltpu.VMEM((tiles // 2, 4, EDGES), F32),
+            pltpu.VMEM((1, width), BF16),
+            pltpu.VMEM((2 * K, count), BF16),
             pltpu.VMEM((half, width), BF16),
             pltpu.VMEM((half, width), BF16),
+            pltpu.VMEM((count, 6 * K), F32),
+            pltpu.VMEM((tiles // 2, 8, EDGES), F32),
+            pltpu.VMEM((tiles, 1, EDGES), jnp.int32),
             dma((band // CH,)),
             dma((2, pieces)),
             dma((2, pieces)),
@@ -308,12 +335,17 @@
             dma((6,)),
             dma,
             dma,
-        ],
+            dma((tiles,)),
+        ]
+        + [pltpu.SMEM((1, EDGES), jnp.int32)] * tiles,
         compiler_params=pltpu.CompilerParams(
             collective_id=0, has_side_effects=True, vmem_limit_bytes=60 * 1024 * 1024
         ),
-    )(grid_latent, idx, bias, mesh_latent, query_weight, key_weight, value_weight, out_weight, gain)
-    return out
+    )(
+        grid_latent, neighbours.T, edge_bias.T, mesh_latent, query_weight, key_weight, value_weight, out_weight,
+        norm_gain.reshape(1, width),
+    )
+    return out.astype(BF16)
 
 
 def solution(mesh):

time: 53.8 us -> 46.3 us (0.86)
  local copies, waits for them, and re-layouts: 5.87 us -> 1.22 us
  Pallas kernels: 45.9 us -> 43 us
    pallas_call x1, Pallas kernels: 45.9 us -> 43 us  [shards(): pl.pallas_call(functools.partial(kernel, lax.axis_size('lat') - 1), out_s...]
    convert_element_type x0 -> x1, other arithmetic: none -> 1.84 us  [shards(): return out.astype(BF16)]
    unnamed x1 -> x0, local copies, waits for them, and re-layouts: 1.72 us -> none
    reshape x4 -> x1, local copies, waits for them, and re-layouts: 2.7 us -> 1.22 us  [shards(): norm_gain.reshape(1, width)]
    broadcast_in_dim x3 -> x0, local copies, waits for them, and re-layouts: 1.42 us -> none  [the longest x1 1.25 us: shards(): gain = jnp.broadcast_to(norm_gain.astype(F32)[None], (8, width))]
    select_n x1 -> x0, other arithmetic: 0.79 us -> none  [shards(): row = jnp.where(neighbours >= 0, row, HALO)]
    ge x1 -> x0, other arithmetic: 0.79 us -> none  [shards(): row = jnp.where(neighbours >= 0, row, HALO)]
where the time goes in v3:
time: 46.3 us; the launch traced here: 46.1 us
  Pallas kernels  43 us (93%)
  other arithmetic  1.84 us (4%)
  local copies, waits for them, and re-layouts  1.22 us (3%)
    pallas_call x1, Pallas kernels, shards(): pl.pallas_call(functools.partial(kernel, lax.axis_size('lat') - 1), out_s...  43 us
    convert_element_type x1, other arithmetic, shards(): return out.astype(BF16)  1.84 us
    reshape x1, local copies, waits for them, and re-layouts, shards(): norm_gain.reshape(1, width)  1.22 us

profile of v3, /device:TPU:97, one launch (start us, length us, event | category | flops | bytes accessed | tf_op | source)
XLA Modules:
  0.0 46.1 jit_solution(14476855473708267835)
XLA Ops:
  0.0 1.2 %reshape.3.gain_ref = bf16[1,256]{1,0:T(2,128)(2,1)} reshape(bf16[256]{0:T(256)(128)(2,1)} %param.17) | data formatting | bytes 1024 | tf_op jit(solution)/shard_map/reshape | solution.py:346
  1.2 43.0 %shard_map.91 = f32[640,256]{1,0:T(8,128)} custom-call(bf16[8192,512]{1,0:T(8,128)(2,1)} %grid_ref.1, s32[16,640]{1,0:T(8,128)} %bitcast.2, bf16[32,640]{1,0:T(8,128)(2,1)} %bitcast.3, bf16[640,512]{1,0:T(8,128)(2,1)} %mesh_ref.1, bf16[512,256]{1,0:T(8,128)(2,1)} %wq_ref.1, bf16[512,256]{1,0:T(8,128)(2,1)} %wk_ref.1, bf16[512,256]{1,0:T(8,128)(2,1)} %wv_ref.1, ...), custom_call_target="tpu_custom_call" | custom-call | tf_op jit(solution)/shard_map/pallas_call | solution.py:303
  44.2 1.8 %convert_element_type.3 = bf16[640,256]{1,0:T(8,128)(2,1)} convert(f32[640,256]{1,0:T(8,128)} %shard_map.91) | non-fusion elementwise | flops 163840 | bytes 983040 | tf_op jit(solution)/shard_map/convert_element_type | solution.py:348

commit v4 on v3

--- a/solution.py
+++ b/solution.py
@@ -28,13 +28,14 @@
 
 
 def kernel(
-    last, grid_ref, nb_ref, bias_ref, mesh_ref, wq_ref, wk_ref, wv_ref, wo_ref, gain_ref, out_ref,
-    buf, hbuf, table, st0, st1, qs, cs, gs, ss, wq2, wk2, wv2, wo2, gain2, bias2, out_send, out_recv,
+    last, grid_ref, nb_in, bias_in, mesh_in, wq_in, wk_in, wv_in, wo_in, gain_in, out_ref,
+    buf, hbuf, table, st0, st1, qs, cs, gs, ss, wq2, wk2, wv2, wo2, gain2, bias2, out_send, out_keep,
+    nb_ref, bias_ref, mesh_ref, wq_ref, wk_ref, wv_ref, wo_ref, gain_ref, local_sem,
     channels, spread, rows_v, load_sem, ici_send, ici_recv, fwd_send, fwd_recv, w_send, w_recv, x_send, x_recv, s_sem,
     *row_refs,
 ):
     band = grid_ref.shape[0]
-    half = mesh_ref.shape[0] // 2
+    half = mesh_in.shape[0] // 2
     tiles = half // TN
     share = HALO // 2
     pieces = share // PIECE
@@ -49,9 +50,6 @@
         pltpu.make_async_copy(grid_ref.at[pl.ds(i * CH, CH), :], buf.at[pl.ds(i * CH, CH), :], load_sem.at[i])
         for i in range(chunks)
     ]
-    for load in loads:
-        load.start()
-
     barrier = pltpu.get_barrier_semaphore()
     pl.semaphore_signal(barrier, inc=1, device_id=(lat, other), device_id_type=MESH)
 
@@ -99,12 +97,12 @@
 
     pairs = tiles // 2
     given = [
-        (wq_ref, wq2),
-        (wk_ref, wk2),
-        (bias_ref, bias2),
-        (wv_ref, wv2),
-        (wo_ref, wo2),
-        (gain_ref, gain2),
+        (wq_in, wq2),
+        (wk_in, wk2),
+        (bias_in, bias2),
+        (wv_in, wv2),
+        (wo_in, wo2),
+        (gain_in, gain2),
     ]
     gifts = [
         pltpu.make_async_remote_copy(
@@ -119,8 +117,23 @@
     ]
     for gift in gifts:
         gift.start()
-
-    mesh_rows = mesh_ref[pl.ds(pl.multiple_of(c * half, half), half), :]
+    mine = [
+        (mesh_in.at[pl.ds(pl.multiple_of(c * half, half), half), :], mesh_ref),
+        (wq_in, wq_ref),
+        (wk_in, wk_ref),
+        (nb_in, nb_ref),
+        (bias_in, bias_ref),
+        (wv_in, wv_ref),
+        (wo_in, wo_ref),
+        (gain_in, gain_ref),
+    ]
+    mine = [pltpu.make_async_copy(source, target, local_sem.at[i]) for i, (source, target) in enumerate(mine)]
+    for load in mine + loads:
+        load.start()
+    for load in mine:
+        load.wait()
+
+    mesh_rows = mesh_ref[...]
 
     def absorbed(part, wq, wk):
         q = jnp.dot(mesh_rows, wq[...], preferred_element_type=F32).astype(BF16)
@@ -261,27 +274,29 @@
             for j in range(2)
         ]
         projected = projected + jnp.dot(jnp.concatenate(attended, axis=1), wo[...], preferred_element_type=F32)
-    updated = mesh_ref[pl.ds(pl.multiple_of(c * half, half), half), :].astype(F32) + projected
+    updated = mesh_ref[...].astype(F32) + projected
     mean = jnp.sum(updated, axis=1, keepdims=True) / D
     variance = jnp.sum(updated * updated, axis=1, keepdims=True) / D - mean * mean
     normed = (updated - mean) * lax.rsqrt(variance + EPSILON)
     left, right = normed[:, 0:D // 2], normed[:, D // 2:D]
     first = c == 0
-    out_send[...] = (jnp.where(first, right, left) * gain2[...].astype(F32)).astype(BF16)
+    gains = [gain_ref[...].astype(F32).reshape(1, D // 2), gain2[...].astype(F32).reshape(1, D // 2)]
+    out_send[...] = (jnp.where(first, right, left) * gains[1]).astype(BF16)
+    out_keep[...] = (jnp.where(first, left, right) * gains[0]).astype(BF16)
+    out_rows = out_ref.at[pl.ds(pl.multiple_of(c * half, half), half), :]
     swap = pltpu.make_async_remote_copy(
         src_ref=out_send,
-        dst_ref=out_recv,
+        dst_ref=out_rows,
         send_sem=x_send,
         recv_sem=x_recv,
         device_id=(lat, other),
         device_id_type=MESH,
     )
-    out_ref[pl.ds(pl.multiple_of(c * half, half), half), :] = (
-        jnp.where(first, left, right) * gain_ref[...].astype(F32)
-    )
     swap.start()
+    keep = pltpu.make_async_copy(out_keep, out_rows, local_sem.at[0])
+    keep.start()
+    keep.wait()
     swap.wait()
-    out_ref[pl.ds(pl.multiple_of(other * half, half), half), :] = out_recv[...].astype(F32)
     for side, has in ((0, has_high), (1, has_low)):
         for i in range(pieces):
 
@@ -302,9 +317,9 @@
     dma = pltpu.SemaphoreType.DMA
     out = pl.pallas_call(
         functools.partial(kernel, lax.axis_size("lat") - 1),
-        out_shape=jax.ShapeDtypeStruct((count, width), F32),
-        in_specs=[ANY] + [VMEM] * 8,
-        out_specs=VMEM,
+        out_shape=jax.ShapeDtypeStruct((count, width), BF16),
+        in_specs=[ANY] * 9,
+        out_specs=ANY,
         scratch_shapes=[
             pltpu.VMEM((band, D), BF16),
             pltpu.VMEM((2, 2, HALO // 2, D), BF16),
@@ -319,10 +334,19 @@
             pltpu.VMEM((D, width), BF16),
             pltpu.VMEM((D, width), BF16),
             pltpu.VMEM((width, D), BF16),
-            pltpu.VMEM((1, width), BF16),
+            pltpu.VMEM((width,), BF16),
             pltpu.VMEM((2 * K, count), BF16),
             pltpu.VMEM((half, width), BF16),
             pltpu.VMEM((half, width), BF16),
+            pltpu.VMEM((K, count), jnp.int32),
+            pltpu.VMEM((2 * K, count), BF16),
+            pltpu.VMEM((half, D), BF16),
+            pltpu.VMEM((D, width), BF16),
+            pltpu.VMEM((D, width), BF16),
+            pltpu.VMEM((D, width), BF16),
+            pltpu.VMEM((width, D), BF16),
+            pltpu.VMEM((width,), BF16),
+            dma((8,)),
             pltpu.VMEM((count, 6 * K), F32),
             pltpu.VMEM((tiles // 2, 8, EDGES), F32),
             pltpu.VMEM((tiles, 1, EDGES), jnp.int32),
@@ -343,9 +367,9 @@
         ),
     )(
         grid_latent, neighbours.T, edge_bias.T, mesh_latent, query_weight, key_weight, value_weight, out_weight,
-        norm_gain.reshape(1, width),
+        norm_gain,
     )
-    return out.astype(BF16)
+    return out
 
 
 def solution(mesh):

time: 46.3 us -> 42.8 us (0.924)
  Pallas kernels: 43 us -> 40.9 us
  other arithmetic: 1.84 us -> 0 us
  local copies, waits for them, and re-layouts: 1.22 us -> 1.72 us
    pallas_call x1, Pallas kernels: 43 us -> 40.9 us  [shards(): pl.pallas_call(functools.partial(kernel, lax.axis_size('lat') - 1), out_s...]
    convert_element_type x1 -> x0, other arithmetic: 1.84 us -> none  [shards(): return out.astype(BF16)]
    unnamed x0 -> x1, local copies, waits for them, and re-layouts: none -> 1.72 us
    reshape x1 -> x0, local copies, waits for them, and re-layouts: 1.22 us -> none  [shards(): norm_gain.reshape(1, width)]
where the time goes in v4:
time: 42.8 us; the launch traced here: 42.6 us
  Pallas kernels  40.9 us (96%)
  local copies, waits for them, and re-layouts  1.72 us (4%)
    pallas_call x1, Pallas kernels, shards(): pl.pallas_call(functools.partial(kernel, lax.axis_size('lat') - 1), out_s...  40.9 us
    unnamed x1, local copies, waits for them, and re-layouts  1.72 us

profile of v4, /device:TPU:97, one launch (start us, length us, event | category | flops | bytes accessed | tf_op | source)
XLA Modules:
  0.0 42.6 jit_solution(8051524261331125096)
XLA Ops:
  0.0 40.9 %shard_map.91 = bf16[640,256]{1,0:T(8,128)(2,1)} custom-call(bf16[8192,512]{1,0:T(8,128)(2,1)} %grid_ref.1, s32[16,640]{1,0:T(8,128)} %bitcast.2, bf16[32,640]{1,0:T(8,128)(2,1)} %bitcast.3, bf16[640,512]{1,0:T(8,128)(2,1)} %mesh_in.1, bf16[512,256]{1,0:T(8,128)(2,1)} %wq_in.1, bf16[512,256]{1,0:T(8,128)(2,1)} %wk_in.1, bf16[512,256]{1,0:T(8,128)(2,1)} %wv_in.1, ...), custom_call_target="tpu_custom_call" | custom-call | tf_op jit(solution)/shard_map/pallas_call | solution.py:318
  40.9 1.7 %copy.11 = bf16[640,256]{1,0:T(8,128)(2,1)} copy(bf16[640,256]{1,0:T(8,128)(2,1)} %shard_map.91) | data formatting | bytes 655360

commit v5 on v4

--- a/solution.py
+++ b/solution.py
@@ -254,18 +254,16 @@
     total = fold(w, jnp.add)
     ss[...] = w * jnp.concatenate([1.0 / total] * blocks, axis=2)
 
-    @pl.loop(0, pairs)
-    def _(i):
+    for i in range(pairs):
         both = ss[i]
         for j in range(2):
             t = 2 * i + j
             rows = [both[part * 4 + j * 2 + h:part * 4 + j * 2 + h + 1] for part in range(2) for h in range(2)]
             pt = jnp.concatenate([jnp.where(same, row, 0.0).astype(BF16) for row in rows], axis=0)
-            g = gs[pl.ds(pl.multiple_of(t * EDGES, EDGES), EDGES), :]
+            g = gs[t * EDGES:(t + 1) * EDGES, :]
             ctx = jnp.dot(pt, g, preferred_element_type=F32)
-            r0 = pl.multiple_of(t * TN, TN)
             for h in range(HEADS):
-                cs[h, pl.ds(r0, TN), :] = ctx[h * TN:(h + 1) * TN].astype(BF16)
+                cs[h, t * TN:(t + 1) * TN, :] = ctx[h * TN:(h + 1) * TN].astype(BF16)
 
     projected = jnp.zeros((half, D), F32)
     for part, (wv, wo) in enumerate(((wv_ref, wo_ref), (wv2, wo2))):

time: 42.8 us -> 41.1 us (0.960)
  Pallas kernels: 40.9 us -> 39.2 us
    pallas_call x1, Pallas kernels: 40.9 us -> 39.2 us  [shards(): pl.pallas_call(functools.partial(kernel, lax.axis_size('lat') - 1), out_s...]
where the time goes in v5:
time: 41.1 us; the launch traced here: 40.9 us
  Pallas kernels  39.2 us (95%)
  local copies, waits for them, and re-layouts  1.72 us (4%)
    pallas_call x1, Pallas kernels, shards(): pl.pallas_call(functools.partial(kernel, lax.axis_size('lat') - 1), out_s...  39.2 us
    unnamed x1, local copies, waits for them, and re-layouts  1.72 us

profile of v5, /device:TPU:97, one launch (start us, length us, event | category | flops | bytes accessed | tf_op | source)
XLA Modules:
  0.0 40.9 jit_solution(2738264975709212329)
XLA Ops:
  0.0 39.2 %shard_map.91 = bf16[640,256]{1,0:T(8,128)(2,1)} custom-call(bf16[8192,512]{1,0:T(8,128)(2,1)} %grid_ref.1, s32[16,640]{1,0:T(8,128)} %bitcast.2, bf16[32,640]{1,0:T(8,128)(2,1)} %bitcast.3, bf16[640,512]{1,0:T(8,128)(2,1)} %mesh_in.1, bf16[512,256]{1,0:T(8,128)(2,1)} %wq_in.1, bf16[512,256]{1,0:T(8,128)(2,1)} %wk_in.1, bf16[512,256]{1,0:T(8,128)(2,1)} %wv_in.1, ...), custom_call_target="tpu_custom_call" | custom-call | tf_op jit(solution)/shard_map/pallas_call | solution.py:316
  39.2 1.7 %copy.11 = bf16[640,256]{1,0:T(8,128)(2,1)} copy(bf16[640,256]{1,0:T(8,128)(2,1)} %shard_map.91) | data formatting | bytes 655360
